TPU v7x, 64 devices: a 2x2x8 block of a 4x4x8 slice. The times are simulated.
64 devices in a mesh: data: 4 (over x, y), seq: 16 (over z, core).
Axes of the slice: x: 2, y: 2, z: 8, core: 2. Of those that a mesh axis runs over, the one named last changes fastest.
The devices are a block of a 4x4x8 slice.
Arguments:
- tokens: bfloat16 [32, 16384, 384], P('data', 'seq'), parts along dimension 0
- lengths: int32 [32], P('data'), parts along dimension 0
- slot_params: bfloat16 [384, 256], replicated
- logit_scale: float32 [1], replicated
- w_in: bfloat16 [128, 384, 1536], P('seq')
- w_out: bfloat16 [128, 1536, 384], P('seq')
Outputs:
- output: bfloat16 [32, 16384, 384], P('data', 'seq'), parts along dimension 0
There are 4 independent parts. A program takes and returns all parts, laid end to end along the dimension named above; an argument that names none is the same for every part.
All inputs are finite; a program needn't handle non-finite values.
Results may differ from a plain program's by a relative error of at most 0.0173106.
Values are sent between devices in bfloat16 or wider.
A program may use at most 768 MiB of HBM per device.

v0:
```python
import jax
import jax.numpy as jnp
from jax import lax
from jax.sharding import PartitionSpec as P


def solution(mesh):
    seq_size = mesh.shape["seq"]

    def shard_body(tok_blk, len_blk, slot_params, logit_scale, w_in_blk, w_out_blk):
        num_rows, tok_count, model_width = tok_blk.shape
        num_slots = slot_params.shape[1]
        own_slots = num_slots // seq_size
        local_experts = w_in_blk.shape[0]
        slots_per = own_slots // local_experts
        shard_idx = lax.axis_index("seq")
        params_f32 = slot_params.astype(jnp.float32)
        col_inv = lax.rsqrt(jnp.sum(params_f32 * params_f32, axis=0, keepdims=True) + 1e-6)
        phi_norm = (params_f32 * (logit_scale[0] * col_inv)).astype(jnp.bfloat16)
        tok_f32 = tok_blk.astype(jnp.float32)
        tok_norm = (tok_f32 * lax.rsqrt(jnp.sum(tok_f32 * tok_f32, axis=-1, keepdims=True) + 1e-6)).astype(jnp.bfloat16)
        logits = jnp.einsum("btd,dn->btn", tok_norm, phi_norm, preferred_element_type=jnp.float32)
        positions = shard_idx * tok_count + jnp.arange(tok_count)
        is_valid = (positions[None, :] < len_blk[:, None])[:, :, None]
        local_max = jnp.max(jnp.where(is_valid, logits, -jnp.inf), axis=1)
        col_max = lax.pmax(local_max, "seq")
        disp_w = jnp.where(is_valid, jnp.exp(logits - col_max[:, None, :]), 0.0)
        col_sum = lax.psum(jnp.sum(disp_w, axis=1), "seq")
        part_sum = jnp.einsum("btn,btd->bnd", disp_w.astype(jnp.bfloat16), tok_blk, preferred_element_type=jnp.float32).astype(jnp.bfloat16)
        slot_sum = lax.psum_scatter(part_sum, "seq", scatter_dimension=1, tiled=True)
        own_sum = lax.dynamic_slice_in_dim(col_sum, shard_idx * own_slots, own_slots, axis=1)
        slot_in = (slot_sum.astype(jnp.float32) / own_sum[:, :, None]).astype(jnp.bfloat16)
        slot_in = slot_in.reshape(num_rows, local_experts, slots_per, model_width)
        hidden = jax.nn.gelu(jnp.einsum("besd,edf->besf", slot_in, w_in_blk, preferred_element_type=jnp.float32)).astype(jnp.bfloat16)
        slot_out = jnp.einsum("besf,efd->besd", hidden, w_out_blk, preferred_element_type=jnp.float32).astype(jnp.bfloat16)
        slot_out = slot_out.reshape(num_rows, own_slots, model_width)
        all_out = lax.all_gather(slot_out, "seq", axis=1, tiled=True)
        combine_w = jax.nn.softmax(logits, axis=-1).astype(jnp.bfloat16)
        mixed = jnp.einsum("btn,bnd->btd", combine_w, all_out, preferred_element_type=jnp.float32).astype(jnp.bfloat16)
        return jnp.where(is_valid, mixed, jnp.zeros_like(mixed))

    return jax.shard_map(
        shard_body,
        mesh=mesh,
        in_specs=(P("data", "seq", None), P("data"), P(None, None), P(None), P("seq", None, None), P("seq", None, None)),
        out_specs=P("data", "seq", None),
        check_vma=False,
    )
```

profile of v0, /device:TPU:21, one launch (start us, length us, event | category | flops | bytes accessed | tf_op | source)
XLA Modules:
  0.0 185.4 jit_solution(11132313278706918939)
XLA Ops:
  6.5 0.0 reduce-scatter.2.cloned.1.call-start
  7.2 1.0 fusion.42
  8.2 4.1 %fusion.1 = f32[8,1024]{1,0:T(8,128)S(1)} fusion(bf16[8,1024,384]{2,1,0:T(8,128)(2,1)} %param.6), kind=kLoop, calls=%fused_computation.3 | loop fusion | flops 9428992 | bytes 6324224 | tf_op jit(solution)/shard_map/reduce_sum | solution.py:21
  12.4 0.7 broadcast_compare_fusion
  13.1 7.9 %select_reduce_fusion = (f32[8,256]{1,0:T(8,128)S(1)}, f32[8,1024,256]{2,1,0:T(8,128)}) fusion(pred[8,1024]{1,0:T(8,128)(4,1)S(1)} %broadcast_compare_fusion, bf16[384,256]{1,0:T(8,128)(2,1)} %param.8, f32[256]{0:T(256)S(1)} %rsqrt_multiply_fusion, bf16[8,1024,384]{2,1,0:T(8,128)(2,1)} %param.6, f32[8,1024]{1,0:T(8,128)S(1)} %add_rsqrt_fusion), kind=kOutput, calls=%fused_computation.10 | convolution fusion | flops 1624537088 | bytes 14926848 | tf_op jit(solution)/shard_map/btd,dn->btn/dot_general | solution.py:22
  21.0 29.3 %pmax.7 = f32[8,256]{1,0:T(8,128)S(1)} all-reduce(f32[8,256]{1,0:T(8,128)S(1)} %get-tuple-element.5), channel_id=1, replica_groups=mesh['data'=4,'seq'=16] {'seq'}, use_global_device_ids=true, to_apply=%region_5.6 | all-reduce | flops 2048 | bytes 16384 | tf_op jit(solution)/shard_map/pmax | solution.py:26
  50.3 7.8 %fusion.22 = bf16[8,256,384]{2,1,0:T(8,128)(2,1)} fusion(bf16[8,1024,384]{2,1,0:T(8,128)(2,1)} %param.6, f32[8,1024,256]{2,1,0:T(8,128)} %get-tuple-element.6, f32[8,256]{1,0:T(8,128)S(1)} %pmax.7, pred[8,1024]{1,0:T(8,128)(4,1)S(1)} %broadcast_compare_fusion), kind=kOutput, calls=%fused_computation.25 | convolution fusion | flops 1617690624 | bytes 16269312 | tf_op jit(solution)/shard_map/btn,btd->bnd/dot_general | solution.py:29
  58.1 0.1 reduce-scatter.2.cloned.1.call-update
  58.2 0.1 all-gather.2.cloned.1.call-start
  58.2 4.8 %fusion.7 = f32[8,256]{1,0:T(8,128)S(1)} fusion(f32[8,1024,256]{2,1,0:T(8,128)} %get-tuple-element.6, f32[8,256]{1,0:T(8,128)S(1)} %pmax.7, pred[8,1024]{1,0:T(8,128)(4,1)S(1)} %broadcast_compare_fusion), kind=kLoop, calls=%fused_computation.13 | loop fusion | flops 6289408 | bytes 8413184 | tf_op jit(solution)/shard_map/reduce_sum | solution.py:28
  63.0 26.8 %psum.7 = f32[8,256]{1,0:T(8,128)S(1)} all-reduce(f32[8,256]{1,0:T(8,128)S(1)} %fusion.7), channel_id=1, replica_groups=mesh['data'=4,'seq'=16] {'seq'}, use_global_device_ids=true, to_apply=%region_8.9 | all-reduce | flops 2048 | bytes 16384 | tf_op jit(solution)/shard_map/psum | solution.py:28
  89.8 0.1 constant_dynamic-slice_fusion
  89.9 20.9 %reduce-scatter.2.cloned.1.call-done = bf16[8,16,384]{2,1,0:T(8,128)(2,1)} async-done(((bf16[8,256,384]{2,1,0:T(8,128)(2,1)}), bf16[8,16,384]{2,1,0:T(8,128)(2,1)}) %reduce-scatter.2.cloned.1.call-update) | async-done | bytes 98320 | tf_op jit(solution)/shard_map/reduce_scatter | solution.py:30
  110.8 1.0 divide_convert_fusion.4
  111.8 8.9 %fusion.25 = bf16[8,8,2,384]{3,1,2,0:T(8,128)(2,1)S(1)} fusion(bf16[8,1536,384]{2,1,0:T(8,128)(2,1)} %param.11, bf16[8,8,2,384]{3,0,2,1:T(8,128)(2,1)S(1)} %bitcast.44, bf16[8,384,1536]{2,1,0:T(8,128)(2,1)} %param.10), kind=kOutput, calls=%fused_computation.27 | convolution fusion | flops 303808512 | bytes 19070976 | tf_op jit(solution)/shard_map/besf,efd->besd/dot_general | solution.py:35
  120.8 0.7 copy.9
  121.4 0.1 all-gather.2.cloned.1.call-update
  121.5 8.0 %fusion.57 = f32[8,1024]{1,0:T(8,128)S(1)} fusion(f32[8,1024,256]{2,1,0:T(8,128)} %get-tuple-element.6), kind=kOutput, calls=%fused_computation.58 | output fusion | flops 4194559 | bytes 8421376 | tf_op jit(solution)/shard_map/sub | solution.py:38
  129.6 29.7 %all-gather.2.cloned.1.call-done = bf16[8,256,384]{2,1,0:T(8,128)(2,1)} async-done(((bf16[8,16,384]{2,1,0:T(8,128)(2,1)}), bf16[8,256,384]{2,1,0:T(8,128)(2,1)}) %all-gather.2.cloned.1.call-update) | async-done | bytes 1572880 | tf_op jit(solution)/shard_map/all_gather | solution.py:37
  159.2 19.3 %convert_select_fusion = bf16[8,1024,384]{2,1,0:T(8,128)(2,1)} fusion(pred[8,1024]{1,0:T(8,128)(4,1)S(1)} %broadcast_compare_fusion, bf16[8,256,384]{2,1,0:T(8,128)(2,1)} %all-gather.2.cloned.1.call-done, f32[8,1024]{1,0:T(8,128)S(1)} %fusion.57, f32[8,1024,256]{2,1,0:T(8,128)} %get-tuple-element.6), kind=kOutput, calls=%fused_computation.16 | convolution fusion | flops 1623204096 | bytes 16293888 | tf_op jit(solution)/shard_map/btn,bnd->btd/dot_general | solution.py:39
  (4 shorter events, 0.0 us)
Async XLA Ops:
  6.5 104.3 %reduce-scatter.2.cloned.1.call-start = ((), (), s32[]{:S(2)}) async-start(), calls=%async_computation.1 | async-start | bytes 1671168 | tf_op jit(solution)/shard_map/reduce_scatter | solution.py:30
  58.2 101.1 %all-gather.2.cloned.1.call-start = ((), (), s32[]{:S(2)}) async-start(), calls=%async_computation.2 | async-start | bytes 1671168 | tf_op jit(solution)/shard_map/all_gather | solution.py:37
Sparse Core Ops, SparseCore 0:
  58.3 52.4 reduce-scatter.1
  121.6 37.5 all-gather.1
where the time goes:
time: 186 us; the launch traced here: 185 us
  blocking collectives  56 us (30%)
  waiting for transfers between devices  50.7 us (27%)
  matrix products  44 us (24%)
  other arithmetic  19.7 us (11%)
  between operations  14.2 us (8%)
    all_gather x1, waiting for transfers between devices, shard_body(): all_out = lax.all_gather(slot_out, 'seq', axis=1, tiled=True)  29.7 us
    pmax x1, blocking collectives, shard_body(): col_max = lax.pmax(local_max, 'seq')  29.3 us
    psum x1, blocking collectives, shard_body(): col_sum = lax.psum(jnp.sum(disp_w, axis=1), 'seq')  26.8 us
    reduce_scatter x1, waiting for transfers between devices, shard_body(): lax.psum_scatter(part_sum, 'seq', scatter_dimension=1, tiled=True)  20.9 us
    dot_general x1, matrix products, shard_body(): jnp.einsum('btn,bnd->btd', combine_w, all_out, preferred_element_type=jnp...  19.3 us
    dot_general x1, matrix products, shard_body(): jnp.einsum('besf,efd->besd', hidden, w_out_blk, preferred_element_type=jn...  8.94 us
    sub x1, other arithmetic, shard_body(): combine_w = jax.nn.softmax(logits, axis=-1).astype(jnp.bfloat16)  8.04 us
    dot_general x1, matrix products, shard_body(): jnp.einsum('btd,dn->btn', tok_norm, phi_norm, preferred_element_type=jnp....  7.94 us
  transfers between devices with their start and end apart: 2, of which 2 were waited for; matrix products, arithmetic and copies ran while one was open for 7% of the time, Pallas kernels for 0%

commit v1 on v0

v1 whole, which is shorter than its diff:
```python
import functools

import jax
import jax.numpy as jnp
from jax import lax
from jax.experimental import pallas as pl
from jax.experimental.pallas import tpu as pltpu
from jax.sharding import PartitionSpec as P

F32 = jnp.float32
BF16 = jnp.bfloat16
MESH = pl.DeviceIdType.MESH
NT = (((1,), (1,)), ((), ()))
UP, DOWN = 0, 1
GROUP_ROWS = 2
HALVES = 2
CORES = 2


def _exchange_kernel(dims, len_ref, scale_ref, phi_ref, tok_ref, win_ref, wout_ref, comb_ref, gat_ref,
                     xbuf, xnbuf, phi_ring, phi_comb, part, pin, chip, sbuf, rbuf, zpart, zpin, zchip, zrecv,
                     slot_in, win, wout, gath, ypart, cbuf,
                     x_sem, win_sem, wout_sem, pr_send, pr_recv, rs_send, rs_recv, z_send, z_recv,
                     ag_send, ag_recv, pg_send, pg_recv, lg_sem, c_sem):
    rows, toks, width, slots, seq, experts, ff = dims
    chips = seq // CORES
    own = slots // seq
    per = own // experts
    groups = rows // GROUP_ROWS
    far = chips // 2
    half_e = experts // HALVES
    hs = own // HALVES
    par = slots // CORES

    me = lax.axis_index("seq")
    z = me // CORES
    core = me % CORES
    other = 1 - core

    def chip_at(delta):
        return (z + delta + chips) % chips

    def dev_at(delta):
        return chip_at(delta) * CORES + core

    partner = z * CORES + other
    up, down = dev_at(1), dev_at(-1)
    target = {UP: up, DOWN: down}

    barrier = pltpu.get_barrier_semaphore()
    for delta in range(1, chips):
        pl.semaphore_signal(barrier, inc=1, device_id={"seq": dev_at(delta)}, device_id_type=MESH)
    pl.semaphore_signal(barrier, inc=1, device_id={"seq": partner}, device_id_type=MESH)

    x_copies = [pltpu.make_async_copy(tok_ref.at[b], xbuf.at[b], x_sem.at[b]) for b in range(rows)]
    for copy in x_copies:
        copy.start()
    w_copies = []
    for h in range(HALVES):
        es = pl.ds(h * half_e, half_e)
        w_copies.append((pltpu.make_async_copy(win_ref.at[es], win.at[es], win_sem.at[h]),
                         pltpu.make_async_copy(wout_ref.at[es], wout.at[es], wout_sem.at[h])))
    for pair in w_copies:
        for copy in pair:
            copy.start()

    gain = scale_ref[0]
    params = phi_ref[...].astype(F32)
    col_inv = lax.rsqrt(jnp.sum(params * params, axis=0, keepdims=True) + 1e-6)
    phi_norm = (params * (gain * col_inv)).astype(BF16).astype(F32)
    phi_t = phi_norm.T
    ring_order = [phi_t[(d * CORES + p) * own:(d * CORES + p + 1) * own] for p in range(CORES) for d in range(chips)]
    phi_ring[...] = jnp.concatenate(ring_order, axis=0).astype(BF16)
    comb_order = [phi_t[i * own + h * hs:i * own + (h + 1) * hs] for h in range(HALVES) for i in range(seq)]
    phi_comb[...] = jnp.concatenate(comb_order, axis=0).astype(BF16)
    bound = gain * 1.01
    zlane = lax.broadcasted_iota(jnp.int32, (slots, 128), 1)
    zpart[...] = jnp.zeros_like(zpart)

    def dispatch_row(b, carry):
        x = xbuf[b]
        xf = x.astype(F32)
        inv = lax.rsqrt(jnp.sum(xf * xf, axis=-1, keepdims=True) + 1e-6)
        xn = (xf * inv).astype(BF16)
        xnbuf[b] = xn
        lt = lax.dot_general(phi_ring[...], xn, NT, preferred_element_type=F32)
        pos = me * toks + lax.broadcasted_iota(jnp.int32, (1, toks), 1)
        w = jnp.where(pos < len_ref[b], jnp.exp(lt - bound), 0.0)
        zsum = jnp.sum(w, axis=1, keepdims=True)
        s = jnp.dot(w.astype(BF16), x, preferred_element_type=F32).astype(BF16)
        for p in range(CORES):
            part[p, b] = s[p * par:(p + 1) * par].reshape(chips, own, width)
        hit = jnp.where(zlane == b, zsum, zpart[...].reshape(slots, 128))
        zpart[...] = hit.reshape(CORES, par, 128)
        return carry

    def combine_row(b):
        slot = b % 2
        if b >= 2:
            pltpu.make_async_copy(cbuf.at[slot], comb_ref.at[b - 2], c_sem.at[slot]).wait()
        logits = lax.dot_general(xnbuf[b], phi_comb[...], NT, preferred_element_type=F32)
        e = jnp.exp(logits)
        total = jnp.sum(e, axis=-1, keepdims=True)
        cbuf[slot] = (e * (1.0 / total)).astype(BF16)
        pltpu.make_async_copy(cbuf.at[slot], comb_ref.at[b], c_sem.at[slot]).start()

    def span(g):
        return pl.ds(g * GROUP_ROWS, GROUP_ROWS)

    def pair_copy(g):
        return pltpu.make_async_remote_copy(
            src_ref=part.at[other, span(g)], dst_ref=pin.at[span(g)], send_sem=pr_send.at[g], recv_sem=pr_recv.at[g],
            device_id={"seq": partner}, device_id_type=MESH)

    def zpair_copy():
        return pltpu.make_async_remote_copy(
            src_ref=zpart.at[other], dst_ref=zpin, send_sem=pr_send.at[groups], recv_sem=pr_recv.at[groups],
            device_id={"seq": partner}, device_id_type=MESH)

    def z_copy(delta):
        return pltpu.make_async_remote_copy(
            src_ref=zchip.at[chip_at(delta)], dst_ref=zrecv.at[delta], send_sem=z_send.at[delta],
            recv_sem=z_recv.at[delta], device_id={"seq": dev_at(delta)}, device_id_type=MESH)

    def steps_of(way, index):
        return far if (index % 2 == 0) == (way == UP) else far - 1

    def sign(way):
        return 1 if way == UP else -1

    def rs_copy(way, g, k):
        if k == steps_of(way, g):
            src = chip.at[span(g), chip_at(sign(way) * k)]
        else:
            src = sbuf.at[way, k, span(g)]
        return pltpu.make_async_remote_copy(
            src_ref=src, dst_ref=rbuf.at[way, k, span(g)], send_sem=rs_send.at[way, g, k], recv_sem=rs_recv.at[way, g, k],
            device_id={"seq": target[way]}, device_id_type=MESH)

    def rs_hop(g, step):
        for way in (UP, DOWN):
            k = steps_of(way, g) - step
            if k < 1:
                continue
            if step:
                rs_copy(way, g, k + 1).wait_recv()
                dest = chip_at(sign(way) * k)
                total = chip[span(g), dest].astype(F32) + rbuf[way, k + 1, span(g)].astype(F32)
                sbuf[way, k, span(g)] = total.astype(BF16)
            rs_copy(way, g, k).start()

    def chip_sum(g):
        pair_copy(g).wait_recv()
        chip[span(g)] = (part[core, span(g)].astype(F32) + pin[span(g)].astype(F32)).astype(BF16)

    for g in range(groups):
        for b in range(g * GROUP_ROWS, (g + 1) * GROUP_ROWS):
            x_copies[b].wait()
        lax.fori_loop(g * GROUP_ROWS, (g + 1) * GROUP_ROWS, dispatch_row, 0)
        if g == 0:
            pl.semaphore_wait(barrier, chips)
        pair_copy(g).start()
        if g == groups - 1:
            zpair_copy().start()
        for step in range(far - 1, 0, -1):
            if 0 <= g - 1 - step:
                rs_hop(g - 1 - step, step)
        if g >= 1:
            chip_sum(g - 1)
            rs_hop(g - 1, 0)

    done = 0
    for r in range(groups, groups + far):
        if r > groups:
            for _ in range(2):
                if done < rows - 1:
                    combine_row(done)
                    done += 1
        for step in range(far - 1, 0, -1):
            g = r - 1 - step
            if 0 <= g < groups:
                rs_hop(g, step)
        if r == groups:
            combine_row(done)
            done += 1
            chip_sum(groups - 1)
            rs_hop(groups - 1, 0)
            zpair_copy().wait_recv()
            zs = zpart[core] + zpin[...]
            zl = lax.broadcasted_iota(jnp.int32, zs.shape, 1)
            hi = zs.astype(BF16).astype(F32)
            mid = (zs - hi).astype(BF16).astype(F32)
            low = zs - hi - mid
            split = jnp.where(zl < rows, hi, 0.0)
            split = split + jnp.where((zl >= rows) & (zl < 2 * rows), pltpu.roll(mid, rows, 1), 0.0)
            split = split + jnp.where((zl >= 2 * rows) & (zl < 3 * rows), pltpu.roll(low, 2 * rows, 1), 0.0)
            zchip[...] = split.astype(BF16).reshape(zchip.shape)
            for delta in range(1, chips):
                z_copy(delta).start()
    while done < rows:
        combine_row(done)
        done += 1

    zsum = zchip[z].astype(F32)
    for delta in range(1, chips):
        z_copy(delta).wait_recv()
        zsum = zsum + zrecv[delta].astype(F32)
    lane = lax.broadcasted_iota(jnp.int32, zsum.shape, 1)
    for g in range(groups):
        rs_copy(UP, g, 1).wait_recv()
        rs_copy(DOWN, g, 1).wait_recv()
        for b in range(g * GROUP_ROWS, (g + 1) * GROUP_ROWS):
            s = chip[b, z].astype(F32) + rbuf[UP, 1, b].astype(F32) + rbuf[DOWN, 1, b].astype(F32)
            mine = (lane % rows == b) & (lane < 3 * rows)
            zb = jnp.sum(jnp.where(mine, zsum, 0.0), axis=-1, keepdims=True)
            slot_in[b * own:(b + 1) * own] = (s / zb).astype(BF16)

    count = rows * own
    i0 = lax.broadcasted_iota(jnp.int32, (count, count), 0)
    i1 = lax.broadcasted_iota(jnp.int32, (count, count), 1)
    rb = rows * per
    src = ((i0 % rb) // per) * own + (i0 // rb) * per + i0 % per
    perm = jnp.where(i1 == src, 1.0, 0.0).astype(BF16)
    by_expert = jnp.dot(perm, slot_in[...], preferred_element_type=F32).astype(BF16)
    hc = half_e * rb
    j0 = lax.broadcasted_iota(jnp.int32, (hc, hc), 0)
    j1 = lax.broadcasted_iota(jnp.int32, (hc, hc), 1)
    back = ((j0 % hs) // per) * rb + (j0 // hs) * per + j0 % per
    unperm = jnp.where(j1 == back, 1.0, 0.0).astype(BF16)

    def ag_copy(way, h, k):
        block = dev_at(-sign(way) * (k - 1))
        return pltpu.make_async_remote_copy(
            src_ref=gath.at[h, :, block], dst_ref=gath.at[h, :, block], send_sem=ag_send.at[way, h, k],
            recv_sem=ag_recv.at[way, h, k], device_id={"seq": target[way]}, device_id_type=MESH)

    def block_copies(h, delta):
        index = delta + far
        block = dev_at(delta)
        remote = pltpu.make_async_remote_copy(
            src_ref=gath.at[h, :, block], dst_ref=gat_ref.at[h, :, block], send_sem=pg_send.at[h, index],
            recv_sem=pg_recv.at[h, index], device_id={"seq": partner}, device_id_type=MESH)
        local = pltpu.make_async_copy(gath.at[h, :, block], gat_ref.at[h, :, block], lg_sem.at[h, index])
        return remote, local

    def publish(h, delta):
        for copy in block_copies(h, delta):
            copy.start()

    def ag_hop(h, k):
        for way in (UP, DOWN):
            if k > 1 and k - 1 <= steps_of(way, h):
                ag_copy(way, h, k - 1).wait_recv()
            if k <= steps_of(way, h):
                ag_copy(way, h, k).start()
        if k == 1:
            publish(h, 0)
        else:
            for way in (UP, DOWN):
                if k - 1 <= steps_of(way, h):
                    publish(h, -sign(way) * (k - 1))

    for h in range(HALVES):
        for copy in w_copies[h]:
            copy.wait()
        for i in range(half_e):
            e = h * half_e + i
            hid = jnp.dot(by_expert[e * rb:(e + 1) * rb], win[e], preferred_element_type=F32)
            hid = jax.nn.gelu(hid).astype(BF16)
            ypart[i * rb:(i + 1) * rb] = jnp.dot(hid, wout[e], preferred_element_type=F32).astype(BF16)
            if h and i == half_e // 2:
                ag_hop(0, 2)
        blk = jnp.dot(unperm, ypart[...], preferred_element_type=F32)
        gath[h, :, me] = blk.reshape(rows, hs, width).astype(BF16)
        ag_hop(h, 1)
    ag_hop(0, 3)
    ag_hop(1, 2)
    ag_hop(0, 4)
    ag_hop(1, 3)
    ag_hop(0, 5)
    ag_hop(1, 4)
    ag_hop(1, 5)

    for h in range(HALVES):
        for delta in range(1 - far, far + 1):
            real = delta
            if delta == far:
                real = -far if steps_of(UP, h) == far else far
            remote, local = block_copies(h, real)
            remote.wait()
            local.wait()
        for way in (UP, DOWN):
            for k in range(1, steps_of(way, h) + 1):
                ag_copy(way, h, k).wait_send()
    for g in range(groups):
        pair_copy(g).wait_send()
        for way in (UP, DOWN):
            for k in range(1, steps_of(way, g) + 1):
                rs_copy(way, g, k).wait_send()
    zpair_copy().wait_send()
    for delta in range(1, chips):
        z_copy(delta).wait_send()
    for b in range(rows - 2, rows):
        pltpu.make_async_copy(cbuf.at[b % 2], comb_ref.at[b], c_sem.at[b % 2]).wait()


def _combine_kernel(len_ref, comb_ref, gat_ref, out_ref):
    b = pl.program_id(0)
    toks = out_ref.shape[1]
    half = gat_ref.shape[2]
    pos = lax.axis_index("seq") * toks + lax.broadcasted_iota(jnp.int32, (toks, 1), 0)
    acc = jnp.dot(comb_ref[0, :, :half], gat_ref[0, 0], preferred_element_type=F32)
    for h in range(1, HALVES):
        acc = acc + jnp.dot(comb_ref[0, :, h * half:(h + 1) * half], gat_ref[h, 0], preferred_element_type=F32)
    out_ref[0] = jnp.where(pos < len_ref[b], acc, 0.0).astype(BF16)


def solution(mesh):
    seq = mesh.shape["seq"]

    def shard_body(tok, lens, params, scale, w_in, w_out):
        rows, toks, width = tok.shape
        slots = params.shape[1]
        experts, _, ff = w_in.shape
        own = slots // seq
        chips = seq // CORES
        groups = rows // GROUP_ROWS
        far = chips // 2
        hs = own // HALVES
        par = slots // CORES
        count = rows * own
        dims = (rows, toks, width, slots, seq, experts, ff)
        dma = pltpu.SemaphoreType.DMA
        any_spec = pl.BlockSpec(memory_space=pl.ANY)
        smem = pl.BlockSpec(memory_space=pltpu.SMEM)
        vmem = pl.BlockSpec(memory_space=pltpu.VMEM)
        comb, gat = pl.pallas_call(
            functools.partial(_exchange_kernel, dims),
            out_shape=(jax.ShapeDtypeStruct((rows, toks, slots), BF16),
                       jax.ShapeDtypeStruct((HALVES, rows, seq, hs, width), BF16)),
            in_specs=[smem, smem, vmem, any_spec, any_spec, any_spec],
            out_specs=(any_spec, any_spec),
            scratch_shapes=[
                pltpu.VMEM((rows, toks, width), BF16),
                pltpu.VMEM((rows, toks, width), BF16),
                pltpu.VMEM((slots, width), BF16),
                pltpu.VMEM((slots, width), BF16),
                pltpu.VMEM((CORES, rows, chips, own, width), BF16),
                pltpu.VMEM((rows, chips, own, width), BF16),
                pltpu.VMEM((rows, chips, own, width), BF16),
                pltpu.VMEM((2, far + 1, rows, own, width), BF16),
                pltpu.VMEM((2, far + 1, rows, own, width), BF16),
                pltpu.VMEM((CORES, par, 128), F32),
                pltpu.VMEM((par, 128), F32),
                pltpu.VMEM((chips, own, 128), BF16),
                pltpu.VMEM((chips, own, 128), BF16),
                pltpu.VMEM((count, width), BF16),
                pltpu.VMEM((experts, width, ff), BF16),
                pltpu.VMEM((experts, ff, width), BF16),
                pltpu.VMEM((HALVES, rows, seq, hs, width), BF16),
                pltpu.VMEM((count // HALVES, width), BF16),
                pltpu.VMEM((2, toks, slots), BF16),
                dma((rows,)), dma((HALVES,)), dma((HALVES,)),
                dma((groups + 1,)), dma((groups + 1,)),
                dma((2, groups, far + 1)), dma((2, groups, far + 1)),
                dma((chips,)), dma((chips,)),
                dma((2, HALVES, far + 1)), dma((2, HALVES, far + 1)),
                dma((HALVES, chips + 1)), dma((HALVES, chips + 1)), dma((HALVES, chips + 1)),
                dma((2,)),
            ],
            compiler_params=pltpu.CompilerParams(
                collective_id=0, has_side_effects=True, vmem_limit_bytes=60 * 1024 * 1024),
            name="exchange",
        )(lens, scale, params, tok, w_in, w_out)
        gat = gat.reshape(HALVES, rows, seq * hs, width)
        return pl.pallas_call(
            _combine_kernel,
            grid=(rows,),
            out_shape=jax.ShapeDtypeStruct((rows, toks, width), BF16),
            in_specs=[smem,
                      pl.BlockSpec((1, toks, slots), lambda b: (b, 0, 0)),
                      pl.BlockSpec((HALVES, 1, seq * hs, width), lambda b: (0, b, 0, 0))],
            out_specs=pl.BlockSpec((1, toks, width), lambda b: (b, 0, 0)),
            compiler_params=pltpu.CompilerParams(dimension_semantics=("arbitrary",)),
            name="combine",
        )(lens, comb, gat)

    return jax.shard_map(
        shard_body,
        mesh=mesh,
        in_specs=(P("data", "seq", None), P("data"), P(None, None), P(None), P("seq", None, None), P("seq", None, None)),
        out_specs=P("data", "seq", None),
        check_vma=False,
    )
```

time: 186 us -> 69.5 us (0.37)
  Pallas kernels: 0 us -> 68.6 us
  blocking collectives: 56 us -> 0 us
  waiting for transfers between devices: 50.7 us -> 0 us
  matrix products: 44 us -> 0 us
  other arithmetic: 19.7 us -> 0 us
  between operations: 14.2 us -> 0.66 us
    pallas_call x0 -> x2, Pallas kernels: none -> 68.6 us  [the longest x1 59.5 us: shard_body(): pl.pallas_call(functools.partial(_exchange_kernel, dims), out_shape=(jax....]
    dot_general x4 -> x0, matrix products: 44 us -> none  [the longest x1 19.3 us: shard_body(): jnp.einsum('btn,bnd->btd', combine_w, all_out, preferred_element_type=jnp...]
    all_gather x1 -> x0, waiting for transfers between devices: 29.7 us -> none  [shard_body(): all_out = lax.all_gather(slot_out, 'seq', axis=1, tiled=True)]
    pmax x1 -> x0, blocking collectives: 29.3 us -> none  [shard_body(): col_max = lax.pmax(local_max, 'seq')]
    psum x1 -> x0, blocking collectives: 26.8 us -> none  [shard_body(): col_sum = lax.psum(jnp.sum(disp_w, axis=1), 'seq')]
    reduce_scatter x1 -> x0, waiting for transfers between devices: 20.9 us -> none  [shard_body(): lax.psum_scatter(part_sum, 'seq', scatter_dimension=1, tiled=True)]
    reduce_sum x3 -> x0, other arithmetic: 9.91 us -> none  [the longest x1 4.79 us: shard_body(): col_sum = lax.psum(jnp.sum(disp_w, axis=1), 'seq')]
    sub x1 -> x0, other arithmetic: 8.04 us -> none  [shard_body(): combine_w = jax.nn.softmax(logits, axis=-1).astype(jnp.bfloat16)]
  transfers between devices with their start and end apart: 2 -> 0, of which waited for: 2 -> 0; matrix products, arithmetic and copies ran while one was open for 7% -> 0% of each run, Pallas kernels for 0% -> 0%
where the time goes in v1:
time: 69.5 us; the launch traced here: 69.2 us
  Pallas kernels  68.6 us (99%)
    pallas_call x1, Pallas kernels, shard_body(): pl.pallas_call(functools.partial(_exchange_kernel, dims), out_shape=(jax....  59.5 us
    pallas_call x1, Pallas kernels, shard_body(): pl.pallas_call(_combine_kernel, grid=(rows,), out_shape=jax.ShapeDtypeStr...  9.09 us

profile of v1, /device:TPU:21, one launch (start us, length us, event | category | flops | bytes accessed | tf_op | source)
XLA Modules:
  0.0 69.2 jit_solution(3278272839107707831)
XLA Ops:
  0.7 59.5 %exchange.1 = (bf16[8,1024,256]{2,1,0:T(8,128)(2,1)}, bf16[2,8,16,8,384]{4,3,2,1,0:T(8,128)(2,1)}) custom-call(s32[8]{0:T(128)} %len_ref.3, f32[1]{0:T(128)S(6)} %copy.7.scale_ref, bf16[384,256]{1,0:T(8,128)(2,1)} %phi_ref.1, bf16[8,1024,384]{2,1,0:T(8,128)(2,1)} %tok_ref.1, bf16[8,384,1536]{2,1,0:T(8,128)(2,1)} %win_ref.1, bf16[8,1536,384]{2,1,0:T(8,128)(2,1)} %wout_ref.1), custom_call_target="tpu_custom_call" | custom-call | tf_op jit(solution)/shard_map/exchange/pallas_call | solution.py:337
  60.1 9.1 %combine.1 = bf16[8,1024,384]{2,1,0:T(8,128)(2,1)} custom-call(s32[8]{0:T(128)} %len_ref.3, bf16[8,1024,256]{2,1,0:T(8,128)(2,1)} %get-tuple-element.7.comb_ref, bf16[2,8,128,384]{3,2,1,0:T(8,128)(2,1)} %bitcast.1), custom_call_target="tpu_custom_call" | custom-call | tf_op jit(solution)/shard_map/combine/pallas_call | solution.py:376

commit v2 on v0

v2 whole, which is shorter than its diff:
```python
import functools

import jax
import jax.numpy as jnp
from jax import lax
from jax.experimental import pallas as pl
from jax.experimental.pallas import tpu as pltpu
from jax.sharding import PartitionSpec as P

F32 = jnp.float32
BF16 = jnp.bfloat16
MESH = pl.DeviceIdType.MESH
NT = (((1,), (1,)), ((), ()))
UP, DOWN = 0, 1
GROUP_ROWS = 2
HALVES = 2
CORES = 2
VMEM_LIMIT = 52 * 1024 * 1024
COMBINE_LIMIT = 20 * 1024 * 1024


def _exchange_kernel(dims, len_ref, scale_ref, phi_ref, tok_ref, win_ref, wout_ref, comb_ref, gat_ref,
                     xbuf, xnbuf, phi_ring, phi_comb, part, pin, chip, cbuf, rbuf, zpart, zpin, zchip, zrecv,
                     slot_in, win, wout, ypart,
                     x_sem, w_sem, pr_send, pr_recv, zp_sem, z_sem, relay_recv, fin_recv, rs_send,
                     ag_recv, ag_send, pg_recv):
    rows, toks, width, slots, seq, experts = dims
    chips = seq // CORES
    own = slots // seq
    per = own // experts
    groups = rows // GROUP_ROWS
    far = chips // 2
    half_e = experts // HALVES
    hs = own // HALVES
    par = slots // CORES

    me = lax.axis_index("seq")
    z = me // CORES
    core = me % CORES
    other = 1 - core
    partner = z * CORES + other

    def chip_at(delta):
        return (z + delta + chips) % chips

    def dev_at(delta):
        return chip_at(delta) * CORES + core

    def sign(way):
        return 1 if way == UP else -1

    def remote(src, dst, send, recv, dev):
        return pltpu.make_async_remote_copy(
            src_ref=src, dst_ref=dst, send_sem=send, recv_sem=recv, device_id={"seq": dev}, device_id_type=MESH)

    def wait_bytes(ref, sem):
        pltpu.make_async_copy(ref, ref, sem).wait()

    x_parts = [pl.ds(0, 1), pl.ds(1, 1), pl.ds(2, rows - 2)]
    x_copies = [pltpu.make_async_copy(tok_ref.at[p], xbuf.at[p], x_sem.at[i]) for i, p in enumerate(x_parts)]
    for copy in x_copies:
        copy.start()

    barrier = pltpu.get_barrier_semaphore()
    for delta in range(1, chips):
        pl.semaphore_signal(barrier, inc=1, device_id={"seq": dev_at(delta)}, device_id_type=MESH)
    pl.semaphore_signal(barrier, inc=1, device_id={"seq": partner}, device_id_type=MESH)

    gain = scale_ref[0]
    params = phi_ref[...].astype(F32)
    col_inv = lax.rsqrt(jnp.sum(params * params, axis=0, keepdims=True) + 1e-6)
    phi_norm = (params * (gain * col_inv)).astype(BF16).astype(F32)
    phi_t = phi_norm.T
    ring_order = [phi_t[(d * CORES + p) * own:(d * CORES + p + 1) * own] for p in range(CORES) for d in range(chips)]
    phi_ring[...] = jnp.concatenate(ring_order, axis=0).astype(BF16)
    comb_order = [phi_t[i * own + h * hs:i * own + (h + 1) * hs] for h in range(HALVES) for i in range(seq)]
    phi_comb[...] = jnp.concatenate(comb_order, axis=0).astype(BF16)
    bound = gain * 1.01
    zlane = lax.broadcasted_iota(jnp.int32, (slots, 128), 1)
    zpart[...] = jnp.zeros_like(zpart)

    def dispatch_row(b):
        x = xbuf[b]
        xf = x.astype(F32)
        inv = lax.rsqrt(jnp.sum(xf * xf, axis=-1, keepdims=True) + 1e-6)
        xn = (xf * inv).astype(BF16)
        xnbuf[b] = xn
        lt = lax.dot_general(phi_ring[...], xn, NT, preferred_element_type=F32)
        pos = me * toks + lax.broadcasted_iota(jnp.int32, (1, toks), 1)
        w = jnp.where(pos < len_ref[b], jnp.exp(lt - bound), 0.0)
        zsum = jnp.sum(w, axis=1, keepdims=True)
        s = jnp.dot(w.astype(BF16), x, preferred_element_type=F32).astype(BF16)
        for p in range(CORES):
            part[p, b] = s[p * par:(p + 1) * par].reshape(chips, own, width)
        hit = jnp.where(zlane == b, zsum, zpart[...].reshape(slots, 128))
        zpart[...] = hit.reshape(CORES, par, 128)

    def combine_row(b):
        logits = lax.dot_general(xnbuf[b], phi_comb[...], NT, preferred_element_type=F32)
        e = jnp.exp(logits)
        total = jnp.sum(e, axis=-1, keepdims=True)
        comb_ref[b] = (e * (1.0 / total)).astype(BF16)

    def span(g):
        return pl.ds(g * GROUP_ROWS, GROUP_ROWS)

    def pair_copy(g):
        return remote(part.at[other, span(g)], pin.at[span(g)], pr_send, pr_recv.at[g], partner)

    def zpair_copy():
        return remote(zpart.at[other], zpin, zp_sem.at[0], zp_sem.at[1], partner)

    def chip_sum(g):
        pair_copy(g).wait_recv()
        chip[span(g)] = (part[core, span(g)].astype(F32) + pin[span(g)].astype(F32)).astype(BF16)

    def is_far(way, index):
        return (index % 2 == 0) == (way == UP)

    def rs_first(g):
        for way in (UP, DOWN):
            s = sign(way)
            relay = relay_recv.at[way, g]
            if is_far(way, g):
                remote(chip.at[span(g), chip_at(far * s)], rbuf.at[way, 0, span(g)], rs_send, relay, dev_at(2 * s)).start()
            remote(chip.at[span(g), chip_at(3 * s)], rbuf.at[way, 1, span(g)], rs_send, relay, dev_at(s)).start()
        for way in (UP, DOWN):
            s = sign(way)
            remote(chip.at[span(g), chip_at(s)], rbuf.at[way, 3, span(g)], rs_send, fin_recv, dev_at(s)).start()

    def rs_relay(g):
        for way in (UP, DOWN):
            s = sign(way)
            first = 0 if is_far(way, g) else 1
            wait_bytes(rbuf.at[way, pl.ds(first, 2 - first), span(g)], relay_recv.at[way, g])
            total = chip[span(g), chip_at(2 * s)].astype(F32)
            for kind in range(first, 2):
                total = total + rbuf[way, kind, span(g)].astype(F32)
            cbuf[way, span(g)] = total.astype(BF16)
            remote(cbuf.at[way, span(g)], rbuf.at[way, 2, span(g)], rs_send, fin_recv, dev_at(2 * s)).start()

    def z_exchange():
        zpair_copy().wait_recv()
        zs = zpart[core] + zpin[...]
        zl = lax.broadcasted_iota(jnp.int32, zs.shape, 1)
        hi = zs.astype(BF16).astype(F32)
        mid = (zs - hi).astype(BF16).astype(F32)
        low = zs - hi - mid
        split = jnp.where(zl < rows, hi, 0.0)
        split = split + jnp.where((zl >= rows) & (zl < 2 * rows), pltpu.roll(mid, rows, 1), 0.0)
        split = split + jnp.where((zl >= 2 * rows) & (zl < 3 * rows), pltpu.roll(low, 2 * rows, 1), 0.0)
        zchip[...] = split.astype(BF16).reshape(zchip.shape)
        for delta in range(1, chips):
            remote(zchip.at[chip_at(delta)], zrecv.at[delta], z_sem.at[0], z_sem.at[1], dev_at(delta)).start()

    def weights(h):
        es = pl.ds(h * half_e, half_e)
        return (pltpu.make_async_copy(win_ref.at[es], win.at[es], w_sem.at[h]),
                pltpu.make_async_copy(wout_ref.at[es], wout.at[es], w_sem.at[h]))

    for b in range(rows):
        if b < len(x_parts):
            with jax.named_scope(f"x{b}"):
                x_copies[b].wait()
        with jax.named_scope(f"disp{b}"):
            dispatch_row(b)
        if b == 1:
            for h in range(HALVES):
                for copy in weights(h):
                    copy.start()
            with jax.named_scope("barrier"):
                pl.semaphore_wait(barrier, chips)
        g = b // GROUP_ROWS
        if b % GROUP_ROWS == GROUP_ROWS - 1:
            pair_copy(g).start()
            if b == rows - 1:
                zpair_copy().start()
        elif g >= 1:
            with jax.named_scope(f"sum{g - 1}"):
                chip_sum(g - 1)
                rs_first(g - 1)
        if b == rows - 2:
            with jax.named_scope("relay0"):
                rs_relay(0)

    def comb(b):
        with jax.named_scope(f"comb{b}"):
            combine_row(b)

    def relay(g):
        with jax.named_scope(f"relay{g}"):
            rs_relay(g)

    comb(0)
    with jax.named_scope(f"sum{groups - 1}"):
        chip_sum(groups - 1)
        rs_first(groups - 1)
    relay(1)
    z_exchange()
    comb(1)
    comb(2)
    relay(2)
    comb(3)
    comb(4)
    relay(3)
    comb(5)
    comb(6)
    comb(7)

    with jax.named_scope("zwait"):
        wait_bytes(zrecv.at[pl.ds(1, chips - 1)], z_sem.at[1])
    with jax.named_scope("finwait"):
        wait_bytes(rbuf.at[:, pl.ds(2, 2)], fin_recv)
    zsum = zchip[z].astype(F32)
    for delta in range(1, chips):
        zsum = zsum + zrecv[delta].astype(F32)
    lane = lax.broadcasted_iota(jnp.int32, zsum.shape, 1)
    for b in range(rows):
        s = chip[b, z].astype(F32)
        for way in (UP, DOWN):
            s = s + (rbuf[way, 2, b].astype(F32) + rbuf[way, 3, b].astype(F32))
        mine = (lane % rows == b) & (lane < 3 * rows)
        zb = jnp.sum(jnp.where(mine, zsum, 0.0), axis=-1, keepdims=True)
        slot_in[b * own:(b + 1) * own] = (s / zb).astype(BF16)

    count = rows * own
    i0 = lax.broadcasted_iota(jnp.int32, (count, count), 0)
    i1 = lax.broadcasted_iota(jnp.int32, (count, count), 1)
    rb = rows * per
    src = ((i0 % rb) // per) * own + (i0 // rb) * per + i0 % per
    perm = jnp.where(i1 == src, 1.0, 0.0).astype(BF16)
    by_expert = jnp.dot(perm, slot_in[...], preferred_element_type=F32).astype(BF16)
    hc = half_e * rb
    j0 = lax.broadcasted_iota(jnp.int32, (hc, hc), 0)
    j1 = lax.broadcasted_iota(jnp.int32, (hc, hc), 1)
    back = ((j0 % hs) // per) * rb + (j0 // hs) * per + j0 % per
    unperm = jnp.where(j1 == back, 1.0, 0.0).astype(BF16)

    def block(h, delta):
        return gat_ref.at[:, h, dev_at(delta)]

    def send(h, delta, way, kind, to):
        remote(block(h, delta), block(h, delta), ag_send, ag_recv.at[h, way, kind], dev_at(to)).start()

    def arrived(h, way, kind):
        with jax.named_scope(f"ag_h{h}_w{way}_k{kind}"):
            wait_bytes(block(h, 0), ag_recv.at[h, way, kind])

    def publish(h, delta):
        remote(block(h, delta), block(h, delta), ag_send, pg_recv, partner).start()

    def ring(h, k):
        for way in (UP, DOWN):
            s = sign(way)
            last = far if is_far(way, h) else far - 1
            if k > 1 and k - 1 <= last:
                arrived(h, way, k - 2)
            if k <= last:
                send(h, -s * (k - 1), way, k - 1, s)
            if k > 1 and k - 1 <= last:
                publish(h, -s * (k - 1))
        if k == 1:
            publish(h, 0)

    def direct(h):
        for way in (UP, DOWN):
            send(h, 0, way, 1, 2 * sign(way))
        for way in (UP, DOWN):
            send(h, 0, way, 0, sign(way))
        publish(h, 0)

    def forward(h):
        for way in (UP, DOWN):
            s = sign(way)
            arrived(h, way, 1)
            if is_far(way, h):
                send(h, -2 * s, way, 3, 2 * s)
            send(h, -2 * s, way, 2, s)
            publish(h, -2 * s)
        for way in (UP, DOWN):
            arrived(h, way, 0)
            publish(h, -sign(way))

    def collect(h):
        for way in (UP, DOWN):
            arrived(h, way, 2)
            publish(h, -3 * sign(way))
        for way in (UP, DOWN):
            if is_far(way, h):
                arrived(h, way, 3)
                publish(h, -far * sign(way))

    for h in range(HALVES):
        with jax.named_scope(f"wwait{h}"):
            wait_bytes(win, w_sem.at[h])
        with jax.named_scope(f"ffn{h}"):
            for i in range(half_e):
                e = h * half_e + i
                hid = jnp.dot(by_expert[e * rb:(e + 1) * rb], win[e], preferred_element_type=F32)
                hid = jax.nn.gelu(hid).astype(BF16)
                ypart[i * rb:(i + 1) * rb] = jnp.dot(hid, wout[e], preferred_element_type=F32).astype(BF16)
            blk = jnp.dot(unperm, ypart[...], preferred_element_type=F32)
            gat_ref[:, h, me] = blk.reshape(rows, hs, width).astype(BF16)
        if h == 0:
            ring(0, 1)
        else:
            direct(1)
    ring(0, 2)
    ring(0, 3)
    forward(1)
    ring(0, 4)
    ring(0, 5)
    collect(1)

    with jax.named_scope("end"):
        wait_bytes(gat_ref.at[:, :, pl.ds(0, chips)], pg_recv)
        wait_bytes(gat_ref.at[:, :, pl.ds(0, seq - 1)], ag_send)
        wait_bytes(pin, pr_send)
        zpair_copy().wait_send()
        wait_bytes(zrecv.at[pl.ds(1, chips - 1)], z_sem.at[0])
        wait_bytes(part.at[0, :, pl.ds(0, chips - 1)], rs_send)


def _combine_kernel(len_ref, comb_ref, gat_ref, out_ref, ybuf, y_sem):
    rows, toks, width = ybuf.shape
    pos = lax.axis_index("seq") * toks + lax.broadcasted_iota(jnp.int32, (toks, 1), 0)

    def out_copy(b):
        return pltpu.make_async_copy(ybuf.at[b], out_ref.at[b], y_sem.at[b])

    for b in range(rows):
        acc = jnp.dot(comb_ref[b], gat_ref[b], preferred_element_type=F32)
        ybuf[b] = jnp.where(pos < len_ref[b], acc, 0.0).astype(BF16)
        out_copy(b).start()
    for b in range(rows):
        out_copy(b).wait()


def solution(mesh):
    seq = mesh.shape["seq"]

    def shard_body(tok, lens, params, scale, w_in, w_out):
        rows, toks, width = tok.shape
        slots = params.shape[1]
        experts, _, ff = w_in.shape
        own = slots // seq
        chips = seq // CORES
        groups = rows // GROUP_ROWS
        hs = own // HALVES
        par = slots // CORES
        count = rows * own
        dims = (rows, toks, width, slots, seq, experts)
        dma = pltpu.SemaphoreType.DMA
        any_spec = pl.BlockSpec(memory_space=pl.ANY)
        smem = pl.BlockSpec(memory_space=pltpu.SMEM)
        vmem = pl.BlockSpec(memory_space=pltpu.VMEM)
        comb, gat = pl.pallas_call(
            functools.partial(_exchange_kernel, dims),
            out_shape=(pltpu.VMEM((rows, toks, slots), BF16),
                       pltpu.VMEM((rows, HALVES, seq, hs, width), BF16)),
            in_specs=[smem, smem, vmem, any_spec, any_spec, any_spec],
            out_specs=(vmem, vmem),
            scratch_shapes=[
                pltpu.VMEM((rows, toks, width), BF16),
                pltpu.VMEM((rows, toks, width), BF16),
                pltpu.VMEM((slots, width), BF16),
                pltpu.VMEM((slots, width), BF16),
                pltpu.VMEM((CORES, rows, chips, own, width), BF16),
                pltpu.VMEM((rows, chips, own, width), BF16),
                pltpu.VMEM((rows, chips, own, width), BF16),
                pltpu.VMEM((2, rows, own, width), BF16),
                pltpu.VMEM((2, 4, rows, own, width), BF16),
                pltpu.VMEM((CORES, par, 128), F32),
                pltpu.VMEM((par, 128), F32),
                pltpu.VMEM((chips, own, 128), BF16),
                pltpu.VMEM((chips, own, 128), BF16),
                pltpu.VMEM((count, width), BF16),
                pltpu.VMEM((experts, width, ff), BF16),
                pltpu.VMEM((experts, ff, width), BF16),
                pltpu.VMEM((count // HALVES, width), BF16),
                dma((3,)), dma((HALVES,)), dma, dma((groups,)), dma((2,)), dma((2,)),
                dma((2, groups)), dma, dma, dma((HALVES, 2, 4)), dma, dma,
            ],
            compiler_params=pltpu.CompilerParams(
                collective_id=0, has_side_effects=True, vmem_limit_bytes=VMEM_LIMIT),
            name="exchange",
        )(lens, scale, params, tok, w_in, w_out)
        gat = gat.reshape(rows, slots, width)
        return pl.pallas_call(
            _combine_kernel,
            out_shape=jax.ShapeDtypeStruct((rows, toks, width), BF16),
            in_specs=[smem, vmem, vmem],
            out_specs=any_spec,
            scratch_shapes=[pltpu.VMEM((rows, toks, width), BF16), dma((rows,))],
            compiler_params=pltpu.CompilerParams(vmem_limit_bytes=COMBINE_LIMIT),
            name="combine",
        )(lens, comb, gat)

    return jax.shard_map(
        shard_body,
        mesh=mesh,
        in_specs=(P("data", "seq", None), P("data"), P(None, None), P(None), P("seq", None, None), P("seq", None, None)),
        out_specs=P("data", "seq", None),
        check_vma=False,
    )
```

time: 186 us -> 51 us (0.27)
  blocking collectives: 56 us -> 0 us
  waiting for transfers between devices: 50.7 us -> 0 us
  Pallas kernels: 0 us -> 50.1 us
  matrix products: 44 us -> 0 us
  other arithmetic: 19.7 us -> 0 us
  between operations: 14.2 us -> 0.84 us
    pallas_call x0 -> x2, Pallas kernels: none -> 50.1 us  [the longest x1 46.2 us: shard_body(): pl.pallas_call(functools.partial(_exchange_kernel, dims), out_shape=(pltp...]
    dot_general x4 -> x0, matrix products: 44 us -> none  [the longest x1 19.3 us: shard_body(): jnp.einsum('btn,bnd->btd', combine_w, all_out, preferred_element_type=jnp...]
    all_gather x1 -> x0, waiting for transfers between devices: 29.7 us -> none  [shard_body(): all_out = lax.all_gather(slot_out, 'seq', axis=1, tiled=True)]
    pmax x1 -> x0, blocking collectives: 29.3 us -> none  [shard_body(): col_max = lax.pmax(local_max, 'seq')]
    psum x1 -> x0, blocking collectives: 26.8 us -> none  [shard_body(): col_sum = lax.psum(jnp.sum(disp_w, axis=1), 'seq')]
    reduce_scatter x1 -> x0, waiting for transfers between devices: 20.9 us -> none  [shard_body(): lax.psum_scatter(part_sum, 'seq', scatter_dimension=1, tiled=True)]
    reduce_sum x3 -> x0, other arithmetic: 9.91 us -> none  [the longest x1 4.79 us: shard_body(): col_sum = lax.psum(jnp.sum(disp_w, axis=1), 'seq')]
    sub x1 -> x0, other arithmetic: 8.04 us -> none  [shard_body(): combine_w = jax.nn.softmax(logits, axis=-1).astype(jnp.bfloat16)]
  transfers between devices with their start and end apart: 2 -> 0, of which waited for: 2 -> 0; matrix products, arithmetic and copies ran while one was open for 7% -> 0% of each run, Pallas kernels for 0% -> 0%
where the time goes in v2:
time: 51 us; the launch traced here: 50.9 us
  Pallas kernels  50.1 us (98%)
  between operations  0.84 us (2%)
    pallas_call x1, Pallas kernels, shard_body(): pl.pallas_call(functools.partial(_exchange_kernel, dims), out_shape=(pltp...  46.2 us
    pallas_call x1, Pallas kernels, shard_body(): pl.pallas_call(_combine_kernel, out_shape=jax.ShapeDtypeStruct((rows, tok...  3.84 us

profile of v2, /device:TPU:21, one launch (start us, length us, event | category | flops | bytes accessed | tf_op | source)
XLA Modules:
  0.0 50.9 jit_solution(8699557762426932746)
XLA Ops:
  0.7 0.0 copy-start
  0.7 46.2 %exchange.1 = (bf16[8,1024,256]{2,1,0:T(8,128)(2,1)S(1)}, bf16[8,2,16,8,384]{4,3,2,1,0:T(8,128)(2,1)S(1)}) custom-call(s32[8]{0:T(128)} %len_ref.3, f32[1]{0:T(128)S(6)} %copy.7.scale_ref, bf16[384,256]{1,0:T(8,128)(2,1)} %phi_ref.1, bf16[8,1024,384]{2,1,0:T(8,128)(2,1)} %tok_ref.1, bf16[8,384,1536]{2,1,0:T(8,128)(2,1)} %win_ref.1, ...), custom_call_target="tpu_custom_call" | custom-call | tf_op jit(solution)/shard_map/exchange/pallas_call | solution.py:357
  46.9 0.0 copy-done
  46.9 3.8 %combine.1 = bf16[8,1024,384]{2,1,0:T(8,128)(2,1)} custom-call(s32[8]{0:T(128)S(1)} %copy-done, bf16[8,1024,256]{2,1,0:T(8,128)(2,1)S(1)} %get-tuple-element.7.comb_ref, bf16[8,256,384]{2,1,0:T(8,128)(2,1)S(1)} %bitcast.1), custom_call_target="tpu_custom_call" | custom-call | tf_op jit(solution)/shard_map/combine/pallas_call | solution.py:389
Async XLA Ops:
  0.7 46.3 %copy-start = (s32[8]{0:T(128)S(1)}, s32[8]{0:T(128)}, u32[]{:S(2)}) copy-start(s32[8]{0:T(128)} %len_ref.3) | copy-start | bytes 100

commit v3 on v2

--- a/solution.py
+++ b/solution.py
@@ -15,14 +15,16 @@
 GROUP_ROWS = 2
 HALVES = 2
 CORES = 2
+RING_GROUPS = 2
+CHUNKS = 2
 VMEM_LIMIT = 52 * 1024 * 1024
 COMBINE_LIMIT = 20 * 1024 * 1024
 
 
 def _exchange_kernel(dims, len_ref, scale_ref, phi_ref, tok_ref, win_ref, wout_ref, comb_ref, gat_ref,
-                     xbuf, xnbuf, phi_ring, phi_comb, part, pin, chip, cbuf, rbuf, zpart, zpin, zchip, zrecv,
+                     xbuf, xnbuf, phi_in, phi_ring, phi_comb, part, pin, chip, cbuf, rbuf, hsend, hrecv, zpart, zpin, zchip, zrecv,
                      slot_in, win, wout, ypart,
-                     x_sem, w_sem, pr_send, pr_recv, zp_sem, z_sem, relay_recv, fin_recv, rs_send,
+                     x_sem, phi_sem, w_sem, pr_send, pr_recv, zp_sem, z_sem, relay_recv, hop_recv, fin_recv, hfin_recv, rs_send,
                      ag_recv, ag_send, pg_recv):
     rows, toks, width, slots, seq, experts = dims
     chips = seq // CORES
@@ -58,6 +60,8 @@
 
     x_parts = [pl.ds(0, 1), pl.ds(1, 1), pl.ds(2, rows - 2)]
     x_copies = [pltpu.make_async_copy(tok_ref.at[p], xbuf.at[p], x_sem.at[i]) for i, p in enumerate(x_parts)]
+    phi_copy = pltpu.make_async_copy(phi_ref, phi_in, phi_sem)
+    phi_copy.start()
     for copy in x_copies:
         copy.start()
 
@@ -66,26 +70,32 @@
         pl.semaphore_signal(barrier, inc=1, device_id={"seq": dev_at(delta)}, device_id_type=MESH)
     pl.semaphore_signal(barrier, inc=1, device_id={"seq": partner}, device_id_type=MESH)
 
+    n0 = lax.broadcasted_iota(jnp.int32, (slots, slots), 0)
+    n1 = lax.broadcasted_iota(jnp.int32, (slots, slots), 1)
+    ring_src = ((n0 % par) // own * CORES + n0 // par) * own + n0 % own
+    comb_src = (n0 % (seq * hs)) // hs * own + n0 // (seq * hs) * hs + n0 % hs
+    ring_hot = jnp.where(n1 == ring_src, 1.0, 0.0).astype(BF16)
+    comb_hot = jnp.where(n1 == comb_src, 1.0, 0.0).astype(BF16)
     gain = scale_ref[0]
-    params = phi_ref[...].astype(F32)
+    with jax.named_scope("phiwait"):
+        phi_copy.wait()
+    params = phi_in[...].astype(F32)
     col_inv = lax.rsqrt(jnp.sum(params * params, axis=0, keepdims=True) + 1e-6)
-    phi_norm = (params * (gain * col_inv)).astype(BF16).astype(F32)
-    phi_t = phi_norm.T
-    ring_order = [phi_t[(d * CORES + p) * own:(d * CORES + p + 1) * own] for p in range(CORES) for d in range(chips)]
-    phi_ring[...] = jnp.concatenate(ring_order, axis=0).astype(BF16)
-    comb_order = [phi_t[i * own + h * hs:i * own + (h + 1) * hs] for h in range(HALVES) for i in range(seq)]
-    phi_comb[...] = jnp.concatenate(comb_order, axis=0).astype(BF16)
+    phi_norm = (params * (gain * col_inv)).astype(BF16)
+    phi_ring[...] = lax.dot_general(ring_hot, phi_norm, NT, preferred_element_type=F32).astype(BF16)
+    phi_comb[...] = lax.dot_general(comb_hot, phi_norm, NT, preferred_element_type=F32).astype(BF16)
     bound = gain * 1.01
     zlane = lax.broadcasted_iota(jnp.int32, (slots, 128), 1)
     zpart[...] = jnp.zeros_like(zpart)
 
+    def normalize_row(b):
+        xf = xbuf[b].astype(F32)
+        inv = lax.rsqrt(jnp.sum(xf * xf, axis=-1, keepdims=True) + 1e-6)
+        xnbuf[b] = (xf * inv).astype(BF16)
+
     def dispatch_row(b):
         x = xbuf[b]
-        xf = x.astype(F32)
-        inv = lax.rsqrt(jnp.sum(xf * xf, axis=-1, keepdims=True) + 1e-6)
-        xn = (xf * inv).astype(BF16)
-        xnbuf[b] = xn
-        lt = lax.dot_general(phi_ring[...], xn, NT, preferred_element_type=F32)
+        lt = lax.dot_general(phi_ring[...], xnbuf[b], NT, preferred_element_type=F32)
         pos = me * toks + lax.broadcasted_iota(jnp.int32, (1, toks), 1)
         w = jnp.where(pos < len_ref[b], jnp.exp(lt - bound), 0.0)
         zsum = jnp.sum(w, axis=1, keepdims=True)
@@ -117,27 +127,51 @@
     def is_far(way, index):
         return (index % 2 == 0) == (way == UP)
 
+    def last_of(way, index):
+        return far if is_far(way, index) else far - 1
+
+    def hop(g, step):
+        for way in (UP, DOWN):
+            s = sign(way)
+            k = last_of(way, g) - step
+            if k < 1:
+                continue
+            if step == 0:
+                src = chip.at[span(g), chip_at(s * k)]
+            else:
+                with jax.named_scope(f"hop{g}_{step}_{way}"):
+                    wait_bytes(hrecv.at[way, k + 1, span(g)], hop_recv.at[way, g, k - 1])
+                total = chip[span(g), chip_at(s * k)].astype(F32) + hrecv[way, k + 1, span(g)].astype(F32)
+                hsend[way, k, span(g)] = total.astype(BF16)
+                src = hsend.at[way, k, span(g)]
+            recv = hfin_recv if k == 1 else hop_recv.at[way, g, k - 2]
+            remote(src, hrecv.at[way, k, span(g)], rs_send, recv, dev_at(s)).start()
+
+    def late(g):
+        return pl.ds((g - RING_GROUPS) * GROUP_ROWS, GROUP_ROWS)
+
     def rs_first(g):
         for way in (UP, DOWN):
             s = sign(way)
-            relay = relay_recv.at[way, g]
+            relay = relay_recv.at[way, g - RING_GROUPS]
             if is_far(way, g):
-                remote(chip.at[span(g), chip_at(far * s)], rbuf.at[way, 0, span(g)], rs_send, relay, dev_at(2 * s)).start()
-            remote(chip.at[span(g), chip_at(3 * s)], rbuf.at[way, 1, span(g)], rs_send, relay, dev_at(s)).start()
-        for way in (UP, DOWN):
-            s = sign(way)
-            remote(chip.at[span(g), chip_at(s)], rbuf.at[way, 3, span(g)], rs_send, fin_recv, dev_at(s)).start()
+                remote(chip.at[span(g), chip_at(far * s)], rbuf.at[way, 0, late(g)], rs_send, relay, dev_at(2 * s)).start()
+            remote(chip.at[span(g), chip_at(3 * s)], rbuf.at[way, 1, late(g)], rs_send, relay, dev_at(s)).start()
+        for way in (UP, DOWN):
+            s = sign(way)
+            remote(chip.at[span(g), chip_at(s)], rbuf.at[way, 3, late(g)], rs_send, fin_recv, dev_at(s)).start()
 
     def rs_relay(g):
         for way in (UP, DOWN):
             s = sign(way)
             first = 0 if is_far(way, g) else 1
-            wait_bytes(rbuf.at[way, pl.ds(first, 2 - first), span(g)], relay_recv.at[way, g])
+            with jax.named_scope(f"relay{g}_{way}"):
+                wait_bytes(rbuf.at[way, pl.ds(first, 2 - first), late(g)], relay_recv.at[way, g - RING_GROUPS])
             total = chip[span(g), chip_at(2 * s)].astype(F32)
             for kind in range(first, 2):
-                total = total + rbuf[way, kind, span(g)].astype(F32)
-            cbuf[way, span(g)] = total.astype(BF16)
-            remote(cbuf.at[way, span(g)], rbuf.at[way, 2, span(g)], rs_send, fin_recv, dev_at(2 * s)).start()
+                total = total + rbuf[way, kind, late(g)].astype(F32)
+            cbuf[way, late(g)] = total.astype(BF16)
+            remote(cbuf.at[way, late(g)], rbuf.at[way, 2, late(g)], rs_send, fin_recv, dev_at(2 * s)).start()
 
     def z_exchange():
         zpair_copy().wait_recv()
@@ -158,67 +192,85 @@
         return (pltpu.make_async_copy(win_ref.at[es], win.at[es], w_sem.at[h]),
                 pltpu.make_async_copy(wout_ref.at[es], wout.at[es], w_sem.at[h]))
 
-    for b in range(rows):
-        if b < len(x_parts):
-            with jax.named_scope(f"x{b}"):
-                x_copies[b].wait()
+    def disp(b):
+        if b + 1 < len(x_parts):
+            with jax.named_scope(f"x{b + 1}"):
+                x_copies[b + 1].wait()
         with jax.named_scope(f"disp{b}"):
+            if b + 1 < rows:
+                normalize_row(b + 1)
             dispatch_row(b)
-        if b == 1:
-            for h in range(HALVES):
-                for copy in weights(h):
-                    copy.start()
-            with jax.named_scope("barrier"):
-                pl.semaphore_wait(barrier, chips)
-        g = b // GROUP_ROWS
-        if b % GROUP_ROWS == GROUP_ROWS - 1:
-            pair_copy(g).start()
-            if b == rows - 1:
-                zpair_copy().start()
-        elif g >= 1:
-            with jax.named_scope(f"sum{g - 1}"):
-                chip_sum(g - 1)
-                rs_first(g - 1)
-        if b == rows - 2:
-            with jax.named_scope("relay0"):
-                rs_relay(0)
 
     def comb(b):
         with jax.named_scope(f"comb{b}"):
             combine_row(b)
 
-    def relay(g):
-        with jax.named_scope(f"relay{g}"):
-            rs_relay(g)
-
+    def total(g):
+        with jax.named_scope(f"sum{g}"):
+            chip_sum(g)
+
+    with jax.named_scope("x0"):
+        x_copies[0].wait()
+    with jax.named_scope("norm0"):
+        normalize_row(0)
+    disp(0)
+    disp(1)
+    for h in range(HALVES):
+        for copy in weights(h):
+            copy.start()
+    disp(2)
+    with jax.named_scope("barrier"):
+        pl.semaphore_wait(barrier, chips)
+    pair_copy(0).start()
+    disp(3)
+    pair_copy(1).start()
+    total(0)
+    hop(0, 0)
+    disp(4)
+    total(1)
+    hop(1, 0)
+    disp(5)
+    pair_copy(2).start()
+    disp(6)
+    hop(0, 1)
+    total(2)
+    rs_first(2)
+    disp(7)
+    pair_copy(3).start()
+    zpair_copy().start()
+    hop(1, 1)
     comb(0)
-    with jax.named_scope(f"sum{groups - 1}"):
-        chip_sum(groups - 1)
-        rs_first(groups - 1)
-    relay(1)
+    total(3)
     z_exchange()
+    rs_first(3)
+    hop(0, 2)
     comb(1)
+    hop(1, 2)
+    rs_relay(2)
     comb(2)
-    relay(2)
+    hop(0, 3)
+    rs_relay(3)
+    hop(1, 3)
     comb(3)
-    comb(4)
-    relay(3)
-    comb(5)
-    comb(6)
-    comb(7)
 
     with jax.named_scope("zwait"):
         wait_bytes(zrecv.at[pl.ds(1, chips - 1)], z_sem.at[1])
-    with jax.named_scope("finwait"):
-        wait_bytes(rbuf.at[:, pl.ds(2, 2)], fin_recv)
     zsum = zchip[z].astype(F32)
     for delta in range(1, chips):
         zsum = zsum + zrecv[delta].astype(F32)
     lane = lax.broadcasted_iota(jnp.int32, zsum.shape, 1)
+    with jax.named_scope("hfin"):
+        wait_bytes(hrecv.at[:, 1], hfin_recv)
+    with jax.named_scope("fin"):
+        wait_bytes(rbuf.at[:, pl.ds(2, 2)], fin_recv)
     for b in range(rows):
         s = chip[b, z].astype(F32)
         for way in (UP, DOWN):
-            s = s + (rbuf[way, 2, b].astype(F32) + rbuf[way, 3, b].astype(F32))
+            if b < RING_GROUPS * GROUP_ROWS:
+                s = s + hrecv[way, 1, b].astype(F32)
+            else:
+                lb = b - RING_GROUPS * GROUP_ROWS
+                s = s + (rbuf[way, 2, lb].astype(F32) + rbuf[way, 3, lb].astype(F32))
         mine = (lane % rows == b) & (lane < 3 * rows)
         zb = jnp.sum(jnp.where(mine, zsum, 0.0), axis=-1, keepdims=True)
         slot_in[b * own:(b + 1) * own] = (s / zb).astype(BF16)
@@ -236,61 +288,67 @@
     back = ((j0 % hs) // per) * rb + (j0 // hs) * per + j0 % per
     unperm = jnp.where(j1 == back, 1.0, 0.0).astype(BF16)
 
-    def block(h, delta):
-        return gat_ref.at[:, h, dev_at(delta)]
-
-    def send(h, delta, way, kind, to):
-        remote(block(h, delta), block(h, delta), ag_send, ag_recv.at[h, way, kind], dev_at(to)).start()
-
-    def arrived(h, way, kind):
-        with jax.named_scope(f"ag_h{h}_w{way}_k{kind}"):
-            wait_bytes(block(h, 0), ag_recv.at[h, way, kind])
-
-    def publish(h, delta):
-        remote(block(h, delta), block(h, delta), ag_send, pg_recv, partner).start()
-
-    def ring(h, k):
-        for way in (UP, DOWN):
-            s = sign(way)
-            last = far if is_far(way, h) else far - 1
+    crows = rows // CHUNKS
+
+    def block(h, c, delta):
+        return gat_ref.at[pl.ds(c * crows, crows), h, dev_at(delta)]
+
+    def send(h, c, delta, way, kind, to):
+        remote(block(h, c, delta), block(h, c, delta), ag_send, ag_recv.at[h, c, way, kind], dev_at(to)).start()
+
+    def arrived(h, c, way, kind):
+        with jax.named_scope(f"ag_h{h}_c{c}_w{way}_k{kind}"):
+            wait_bytes(block(h, c, 0), ag_recv.at[h, c, way, kind])
+
+    def publish(h, c, delta):
+        remote(block(h, c, delta), block(h, c, delta), ag_send, pg_recv, partner).start()
+
+    def ring(c, k):
+        for way in (UP, DOWN):
+            s = sign(way)
+            last = last_of(way, c)
             if k > 1 and k - 1 <= last:
-                arrived(h, way, k - 2)
+                arrived(0, c, way, k - 2)
             if k <= last:
-                send(h, -s * (k - 1), way, k - 1, s)
+                send(0, c, -s * (k - 1), way, k - 1, s)
             if k > 1 and k - 1 <= last:
-                publish(h, -s * (k - 1))
+                publish(0, c, -s * (k - 1))
         if k == 1:
-            publish(h, 0)
-
-    def direct(h):
-        for way in (UP, DOWN):
-            send(h, 0, way, 1, 2 * sign(way))
-        for way in (UP, DOWN):
-            send(h, 0, way, 0, sign(way))
-        publish(h, 0)
-
-    def forward(h):
-        for way in (UP, DOWN):
-            s = sign(way)
-            arrived(h, way, 1)
-            if is_far(way, h):
-                send(h, -2 * s, way, 3, 2 * s)
-            send(h, -2 * s, way, 2, s)
-            publish(h, -2 * s)
-        for way in (UP, DOWN):
-            arrived(h, way, 0)
-            publish(h, -sign(way))
-
-    def collect(h):
-        for way in (UP, DOWN):
-            arrived(h, way, 2)
-            publish(h, -3 * sign(way))
-        for way in (UP, DOWN):
-            if is_far(way, h):
-                arrived(h, way, 3)
-                publish(h, -far * sign(way))
-
-    for h in range(HALVES):
+            publish(0, c, 0)
+
+    def direct_far(c):
+        for way in (UP, DOWN):
+            send(1, c, 0, way, 1, 2 * sign(way))
+
+    def direct_near(c):
+        for way in (UP, DOWN):
+            send(1, c, 0, way, 0, sign(way))
+        publish(1, c, 0)
+
+    def forward(c):
+        for way in (UP, DOWN):
+            s = sign(way)
+            arrived(1, c, way, 1)
+            if is_far(way, c):
+                send(1, c, -2 * s, way, 3, 2 * s)
+            send(1, c, -2 * s, way, 2, s)
+            publish(1, c, -2 * s)
+
+    def near(c):
+        for way in (UP, DOWN):
+            arrived(1, c, way, 0)
+            publish(1, c, -sign(way))
+
+    def collect(c):
+        for way in (UP, DOWN):
+            arrived(1, c, way, 2)
+            publish(1, c, -3 * sign(way))
+        for way in (UP, DOWN):
+            if is_far(way, c):
+                arrived(1, c, way, 3)
+                publish(1, c, -far * sign(way))
+
+    def expert_half(h):
         with jax.named_scope(f"wwait{h}"):
             wait_bytes(win, w_sem.at[h])
         with jax.named_scope(f"ffn{h}"):
@@ -301,16 +359,33 @@
                 ypart[i * rb:(i + 1) * rb] = jnp.dot(hid, wout[e], preferred_element_type=F32).astype(BF16)
             blk = jnp.dot(unperm, ypart[...], preferred_element_type=F32)
             gat_ref[:, h, me] = blk.reshape(rows, hs, width).astype(BF16)
-        if h == 0:
-            ring(0, 1)
-        else:
-            direct(1)
+
+    expert_half(0)
+    ring(0, 1)
+    ring(1, 1)
+    expert_half(1)
+    direct_far(0)
+    direct_far(1)
+    comb(4)
     ring(0, 2)
+    ring(1, 2)
+    direct_near(0)
+    direct_near(1)
+    comb(5)
+    forward(0)
+    forward(1)
     ring(0, 3)
-    forward(1)
+    ring(1, 3)
+    comb(6)
+    near(0)
+    near(1)
+    comb(7)
     ring(0, 4)
+    ring(1, 4)
+    collect(0)
+    collect(1)
     ring(0, 5)
-    collect(1)
+    ring(1, 5)
 
     with jax.named_scope("end"):
         wait_bytes(gat_ref.at[:, :, pl.ds(0, chips)], pg_recv)
@@ -346,6 +421,8 @@
         own = slots // seq
         chips = seq // CORES
         groups = rows // GROUP_ROWS
+        ring_rows = RING_GROUPS * GROUP_ROWS
+        far = chips // 2
         hs = own // HALVES
         par = slots // CORES
         count = rows * own
@@ -358,18 +435,21 @@
             functools.partial(_exchange_kernel, dims),
             out_shape=(pltpu.VMEM((rows, toks, slots), BF16),
                        pltpu.VMEM((rows, HALVES, seq, hs, width), BF16)),
-            in_specs=[smem, smem, vmem, any_spec, any_spec, any_spec],
+            in_specs=[smem, smem, any_spec, any_spec, any_spec, any_spec],
             out_specs=(vmem, vmem),
             scratch_shapes=[
                 pltpu.VMEM((rows, toks, width), BF16),
                 pltpu.VMEM((rows, toks, width), BF16),
+                pltpu.VMEM((width, slots), BF16),
                 pltpu.VMEM((slots, width), BF16),
                 pltpu.VMEM((slots, width), BF16),
                 pltpu.VMEM((CORES, rows, chips, own, width), BF16),
                 pltpu.VMEM((rows, chips, own, width), BF16),
                 pltpu.VMEM((rows, chips, own, width), BF16),
-                pltpu.VMEM((2, rows, own, width), BF16),
-                pltpu.VMEM((2, 4, rows, own, width), BF16),
+                pltpu.VMEM((2, rows - ring_rows, own, width), BF16),
+                pltpu.VMEM((2, 4, rows - ring_rows, own, width), BF16),
+                pltpu.VMEM((2, far, ring_rows, own, width), BF16),
+                pltpu.VMEM((2, far + 1, ring_rows, own, width), BF16),
                 pltpu.VMEM((CORES, par, 128), F32),
                 pltpu.VMEM((par, 128), F32),
                 pltpu.VMEM((chips, own, 128), BF16),
@@ -378,8 +458,9 @@
                 pltpu.VMEM((experts, width, ff), BF16),
                 pltpu.VMEM((experts, ff, width), BF16),
                 pltpu.VMEM((count // HALVES, width), BF16),
-                dma((3,)), dma((HALVES,)), dma, dma((groups,)), dma((2,)), dma((2,)),
-                dma((2, groups)), dma, dma, dma((HALVES, 2, 4)), dma, dma,
+                dma((3,)), dma, dma((HALVES,)), dma, dma((groups,)), dma((2,)), dma((2,)),
+                dma((2, groups - RING_GROUPS)), dma((2, RING_GROUPS, far - 1)), dma, dma, dma,
+                dma((HALVES, CHUNKS, 2, 4)), dma, dma,
             ],
             compiler_params=pltpu.CompilerParams(
                 collective_id=0, has_side_effects=True, vmem_limit_bytes=VMEM_LIMIT),

time: 51 us -> 51 us (level)
  no operation moved by 1% of the time
where the time goes in v3:
time: 51 us; the launch traced here: 50.9 us
  Pallas kernels  50.1 us (98%)
  between operations  0.84 us (2%)
    pallas_call x1, Pallas kernels, shard_body(): pl.pallas_call(functools.partial(_exchange_kernel, dims), out_shape=(pltp...  46.2 us
    pallas_call x1, Pallas kernels, shard_body(): pl.pallas_call(_combine_kernel, out_shape=jax.ShapeDtypeStruct((rows, tok...  3.84 us

profile of v3, /device:TPU:21, one launch (start us, length us, event | category | flops | bytes accessed | tf_op | source)
XLA Modules:
  0.0 50.9 jit_solution(12461258010345543308)
XLA Ops:
  0.7 0.0 copy-start
  0.7 46.2 %exchange.1 = (bf16[8,1024,256]{2,1,0:T(8,128)(2,1)S(1)}, bf16[8,2,16,8,384]{4,3,2,1,0:T(8,128)(2,1)S(1)}) custom-call(s32[8]{0:T(128)} %len_ref.3, f32[1]{0:T(128)S(6)} %copy.7.scale_ref, bf16[384,256]{1,0:T(8,128)(2,1)} %phi_ref.1, bf16[8,1024,384]{2,1,0:T(8,128)(2,1)} %tok_ref.1, bf16[8,384,1536]{2,1,0:T(8,128)(2,1)} %win_ref.1, ...), custom_call_target="tpu_custom_call" | custom-call | tf_op jit(solution)/shard_map/exchange/pallas_call | solution.py:434
  46.9 0.0 copy-done
  46.9 3.8 %combine.1 = bf16[8,1024,384]{2,1,0:T(8,128)(2,1)} custom-call(s32[8]{0:T(128)S(1)} %copy-done, bf16[8,1024,256]{2,1,0:T(8,128)(2,1)S(1)} %get-tuple-element.7.comb_ref, bf16[8,256,384]{2,1,0:T(8,128)(2,1)S(1)} %bitcast.1), custom_call_target="tpu_custom_call" | custom-call | tf_op jit(solution)/shard_map/combine/pallas_call | solution.py:470
Async XLA Ops:
  0.7 46.2 %copy-start = (s32[8]{0:T(128)S(1)}, s32[8]{0:T(128)}, u32[]{:S(2)}) copy-start(s32[8]{0:T(128)} %len_ref.3) | copy-start | bytes 100

commit v4 on v3

--- a/solution.py
+++ b/solution.py
@@ -15,15 +15,27 @@
 GROUP_ROWS = 2
 HALVES = 2
 CORES = 2
-RING_GROUPS = 2
 CHUNKS = 2
+RS_PLAN = "TTTT"
+ORDER = (
+    ("disp", 0), ("disp", 1), ("bar",), ("disp", 2), ("pair", 0), ("disp", 3), ("disp", 4), ("pair", 1),
+    ("total", 0), ("first", 0), ("disp", 5), ("disp", 6), ("pair", 2), ("total", 1), ("first", 1), ("disp", 7),
+    ("disp", 8), ("total", 2), ("first", 2), ("pair", 3), ("total", 3), ("zpair",), ("first", 3), ("relay", 0),
+    ("z",), ("comb", 0), ("comb", 1), ("comb", 2), ("relay", 2), ("relay", 1), ("comb", 3), ("relay", 3),
+    ("comb", 4), ("comb", 5), ("FIN",), ("ffn", 0), ("ring", 0, 0, 1), ("dnear", 0, 1), ("dfar", 0, 1),
+    ("ffn", 1), ("dfar", 1, 1), ("ring", 0, 0, 2), ("dfar", 1, 0), ("dnear", 1, 1), ("comb", 6),
+    ("dnear", 1, 0), ("near", 0, 1), ("comb", 7), ("ring", 0, 0, 3), ("fwd", 1, 1), ("fwd", 0, 1),
+    ("near", 1, 1), ("fwd", 1, 0), ("near", 1, 0), ("ring", 0, 0, 4), ("coll", 1, 1), ("coll", 0, 1),
+    ("ring", 0, 0, 5), ("coll", 1, 0),
+)
+PARTS = 1
 VMEM_LIMIT = 52 * 1024 * 1024
 COMBINE_LIMIT = 20 * 1024 * 1024
 
 
 def _exchange_kernel(dims, len_ref, scale_ref, phi_ref, tok_ref, win_ref, wout_ref, comb_ref, gat_ref,
                      xbuf, xnbuf, phi_in, phi_ring, phi_comb, part, pin, chip, cbuf, rbuf, hsend, hrecv, zpart, zpin, zchip, zrecv,
-                     slot_in, win, wout, ypart,
+                     slot_in, by_expert, win, wout, ypart, wbuf,
                      x_sem, phi_sem, w_sem, pr_send, pr_recv, zp_sem, z_sem, relay_recv, hop_recv, fin_recv, hfin_recv, rs_send,
                      ag_recv, ag_send, pg_recv):
     rows, toks, width, slots, seq, experts = dims
@@ -33,6 +45,7 @@
     groups = rows // GROUP_ROWS
     far = chips // 2
     half_e = experts // HALVES
+    ring_groups = RS_PLAN.count("R")
     hs = own // HALVES
     par = slots // CORES
 
@@ -58,12 +71,12 @@
     def wait_bytes(ref, sem):
         pltpu.make_async_copy(ref, ref, sem).wait()
 
-    x_parts = [pl.ds(0, 1), pl.ds(1, 1), pl.ds(2, rows - 2)]
-    x_copies = [pltpu.make_async_copy(tok_ref.at[p], xbuf.at[p], x_sem.at[i]) for i, p in enumerate(x_parts)]
+    x_parts = {0: pl.ds(0, 1), 1: pl.ds(1, 1), 2: pl.ds(2, 2), 4: pl.ds(4, rows - 4)}
+    x_copies = {b: pltpu.make_async_copy(tok_ref.at[p], xbuf.at[p], x_sem.at[i]) for i, (b, p) in enumerate(x_parts.items())}
     phi_copy = pltpu.make_async_copy(phi_ref, phi_in, phi_sem)
     phi_copy.start()
-    for copy in x_copies:
-        copy.start()
+    x_copies[0].start()
+    x_copies[1].start()
 
     barrier = pltpu.get_barrier_semaphore()
     for delta in range(1, chips):
@@ -79,6 +92,8 @@
     gain = scale_ref[0]
     with jax.named_scope("phiwait"):
         phi_copy.wait()
+    x_copies[2].start()
+    x_copies[4].start()
     params = phi_in[...].astype(F32)
     col_inv = lax.rsqrt(jnp.sum(params * params, axis=0, keepdims=True) + 1e-6)
     phi_norm = (params * (gain * col_inv)).astype(BF16)
@@ -88,22 +103,37 @@
     zlane = lax.broadcasted_iota(jnp.int32, (slots, 128), 1)
     zpart[...] = jnp.zeros_like(zpart)
 
-    def normalize_row(b):
-        xf = xbuf[b].astype(F32)
+    def normalize_part(b, ts):
+        xf = xbuf[b, ts].astype(F32)
         inv = lax.rsqrt(jnp.sum(xf * xf, axis=-1, keepdims=True) + 1e-6)
-        xnbuf[b] = (xf * inv).astype(BF16)
-
-    def dispatch_row(b):
-        x = xbuf[b]
-        lt = lax.dot_general(phi_ring[...], xnbuf[b], NT, preferred_element_type=F32)
-        pos = me * toks + lax.broadcasted_iota(jnp.int32, (1, toks), 1)
-        w = jnp.where(pos < len_ref[b], jnp.exp(lt - bound), 0.0)
-        zsum = jnp.sum(w, axis=1, keepdims=True)
-        s = jnp.dot(w.astype(BF16), x, preferred_element_type=F32).astype(BF16)
-        for p in range(CORES):
-            part[p, b] = s[p * par:(p + 1) * par].reshape(chips, own, width)
-        hit = jnp.where(zlane == b, zsum, zpart[...].reshape(slots, 128))
-        zpart[...] = hit.reshape(CORES, par, 128)
+        xnbuf[b, ts] = (xf * inv).astype(BF16)
+
+    def dispatch_stage(r):
+        tile = toks // PARTS
+        zs = jnp.zeros((slots, 128), F32)
+        cut = -(-width // (256 * PARTS)) * 256
+        for c in range(PARTS):
+            ts = pl.ds(c * tile, tile)
+            if r < rows:
+                lt = lax.dot_general(phi_ring[...], xnbuf[r, ts], NT, preferred_element_type=F32)
+            if r >= 1:
+                lo, hi = min(c * cut, width), min((c + 1) * cut, width)
+                if lo < hi:
+                    s = jnp.dot(wbuf[(r - 1) % 2], xbuf[r - 1, :, lo:hi], preferred_element_type=F32).astype(BF16)
+                    for p in range(CORES):
+                        part[p, r - 1, :, :, lo:hi] = s[p * par:(p + 1) * par].reshape(chips, own, hi - lo)
+            if r + 1 < rows:
+                normalize_part(r + 1, ts)
+            if r < rows:
+                pos = me * toks + c * tile + lax.broadcasted_iota(jnp.int32, (1, tile), 1)
+                w = jnp.exp(lt - jnp.where(pos < len_ref[r], bound, 1e30))
+                for i in range(tile // 128):
+                    zs = zs + w[:, i * 128:(i + 1) * 128]
+                wbuf[r % 2, :, ts] = w.astype(BF16)
+        if r < rows:
+            zsum = jnp.sum(zs, axis=1, keepdims=True)
+            hit = jnp.where(zlane == r, zsum, zpart[...].reshape(slots, 128))
+            zpart[...] = hit.reshape(CORES, par, 128)
 
     def combine_row(b):
         logits = lax.dot_general(xnbuf[b], phi_comb[...], NT, preferred_element_type=F32)
@@ -148,12 +178,12 @@
             remote(src, hrecv.at[way, k, span(g)], rs_send, recv, dev_at(s)).start()
 
     def late(g):
-        return pl.ds((g - RING_GROUPS) * GROUP_ROWS, GROUP_ROWS)
+        return pl.ds((g - ring_groups) * GROUP_ROWS, GROUP_ROWS)
 
     def rs_first(g):
         for way in (UP, DOWN):
             s = sign(way)
-            relay = relay_recv.at[way, g - RING_GROUPS]
+            relay = relay_recv.at[way, g - ring_groups]
             if is_far(way, g):
                 remote(chip.at[span(g), chip_at(far * s)], rbuf.at[way, 0, late(g)], rs_send, relay, dev_at(2 * s)).start()
             remote(chip.at[span(g), chip_at(3 * s)], rbuf.at[way, 1, late(g)], rs_send, relay, dev_at(s)).start()
@@ -166,7 +196,7 @@
             s = sign(way)
             first = 0 if is_far(way, g) else 1
             with jax.named_scope(f"relay{g}_{way}"):
-                wait_bytes(rbuf.at[way, pl.ds(first, 2 - first), late(g)], relay_recv.at[way, g - RING_GROUPS])
+                wait_bytes(rbuf.at[way, pl.ds(first, 2 - first), late(g)], relay_recv.at[way, g - ring_groups])
             total = chip[span(g), chip_at(2 * s)].astype(F32)
             for kind in range(first, 2):
                 total = total + rbuf[way, kind, late(g)].astype(F32)
@@ -193,13 +223,15 @@
                 pltpu.make_async_copy(wout_ref.at[es], wout.at[es], w_sem.at[h]))
 
     def disp(b):
-        if b + 1 < len(x_parts):
+        if b + 1 in x_parts:
             with jax.named_scope(f"x{b + 1}"):
                 x_copies[b + 1].wait()
         with jax.named_scope(f"disp{b}"):
-            if b + 1 < rows:
-                normalize_row(b + 1)
-            dispatch_row(b)
+            dispatch_stage(b)
+        if b == 1:
+            for h in range(HALVES):
+                for copy in weights(h):
+                    copy.start()
 
     def comb(b):
         with jax.named_scope(f"comb{b}"):
@@ -209,71 +241,9 @@
         with jax.named_scope(f"sum{g}"):
             chip_sum(g)
 
-    with jax.named_scope("x0"):
-        x_copies[0].wait()
-    with jax.named_scope("norm0"):
-        normalize_row(0)
-    disp(0)
-    disp(1)
-    for h in range(HALVES):
-        for copy in weights(h):
-            copy.start()
-    disp(2)
-    with jax.named_scope("barrier"):
-        pl.semaphore_wait(barrier, chips)
-    pair_copy(0).start()
-    disp(3)
-    pair_copy(1).start()
-    total(0)
-    hop(0, 0)
-    disp(4)
-    total(1)
-    hop(1, 0)
-    disp(5)
-    pair_copy(2).start()
-    disp(6)
-    hop(0, 1)
-    total(2)
-    rs_first(2)
-    disp(7)
-    pair_copy(3).start()
-    zpair_copy().start()
-    hop(1, 1)
-    comb(0)
-    total(3)
-    z_exchange()
-    rs_first(3)
-    hop(0, 2)
-    comb(1)
-    hop(1, 2)
-    rs_relay(2)
-    comb(2)
-    hop(0, 3)
-    rs_relay(3)
-    hop(1, 3)
-    comb(3)
-
-    with jax.named_scope("zwait"):
-        wait_bytes(zrecv.at[pl.ds(1, chips - 1)], z_sem.at[1])
-    zsum = zchip[z].astype(F32)
-    for delta in range(1, chips):
-        zsum = zsum + zrecv[delta].astype(F32)
-    lane = lax.broadcasted_iota(jnp.int32, zsum.shape, 1)
-    with jax.named_scope("hfin"):
-        wait_bytes(hrecv.at[:, 1], hfin_recv)
-    with jax.named_scope("fin"):
-        wait_bytes(rbuf.at[:, pl.ds(2, 2)], fin_recv)
-    for b in range(rows):
-        s = chip[b, z].astype(F32)
-        for way in (UP, DOWN):
-            if b < RING_GROUPS * GROUP_ROWS:
-                s = s + hrecv[way, 1, b].astype(F32)
-            else:
-                lb = b - RING_GROUPS * GROUP_ROWS
-                s = s + (rbuf[way, 2, lb].astype(F32) + rbuf[way, 3, lb].astype(F32))
-        mine = (lane % rows == b) & (lane < 3 * rows)
-        zb = jnp.sum(jnp.where(mine, zsum, 0.0), axis=-1, keepdims=True)
-        slot_in[b * own:(b + 1) * own] = (s / zb).astype(BF16)
+    def greet():
+        with jax.named_scope("barrier"):
+            pl.semaphore_wait(barrier, chips)
 
     count = rows * own
     i0 = lax.broadcasted_iota(jnp.int32, (count, count), 0)
@@ -281,13 +251,37 @@
     rb = rows * per
     src = ((i0 % rb) // per) * own + (i0 // rb) * per + i0 % per
     perm = jnp.where(i1 == src, 1.0, 0.0).astype(BF16)
-    by_expert = jnp.dot(perm, slot_in[...], preferred_element_type=F32).astype(BF16)
     hc = half_e * rb
     j0 = lax.broadcasted_iota(jnp.int32, (hc, hc), 0)
     j1 = lax.broadcasted_iota(jnp.int32, (hc, hc), 1)
     back = ((j0 % hs) // per) * rb + (j0 // hs) * per + j0 % per
     unperm = jnp.where(j1 == back, 1.0, 0.0).astype(BF16)
 
+    def own_inputs():
+        with jax.named_scope("zwait"):
+            wait_bytes(zrecv.at[pl.ds(1, chips - 1)], z_sem.at[1])
+        zsum = zchip[z].astype(F32)
+        for delta in range(1, chips):
+            zsum = zsum + zrecv[delta].astype(F32)
+        lane = lax.broadcasted_iota(jnp.int32, zsum.shape, 1)
+        if ring_groups:
+            with jax.named_scope("hfin"):
+                wait_bytes(hrecv.at[:, 1], hfin_recv)
+        with jax.named_scope("fin"):
+            wait_bytes(rbuf.at[:, pl.ds(2, 2)], fin_recv)
+        for b in range(rows):
+            s = chip[b, z].astype(F32)
+            for way in (UP, DOWN):
+                if b < ring_groups * GROUP_ROWS:
+                    s = s + hrecv[way, 1, b].astype(F32)
+                else:
+                    lb = b - ring_groups * GROUP_ROWS
+                    s = s + (rbuf[way, 2, lb].astype(F32) + rbuf[way, 3, lb].astype(F32))
+            mine = (lane % rows == b) & (lane < 3 * rows)
+            zb = jnp.sum(jnp.where(mine, zsum, 0.0), axis=-1, keepdims=True)
+            slot_in[b * own:(b + 1) * own] = (s / zb).astype(BF16)
+        by_expert[...] = jnp.dot(perm, slot_in[...], preferred_element_type=F32).astype(BF16)
+
     crows = rows // CHUNKS
 
     def block(h, c, delta):
@@ -303,50 +297,50 @@
     def publish(h, c, delta):
         remote(block(h, c, delta), block(h, c, delta), ag_send, pg_recv, partner).start()
 
-    def ring(c, k):
+    def ring(h, c, k):
         for way in (UP, DOWN):
             s = sign(way)
             last = last_of(way, c)
             if k > 1 and k - 1 <= last:
-                arrived(0, c, way, k - 2)
+                arrived(h, c, way, k - 2)
             if k <= last:
-                send(0, c, -s * (k - 1), way, k - 1, s)
+                send(h, c, -s * (k - 1), way, k - 1, s)
             if k > 1 and k - 1 <= last:
-                publish(0, c, -s * (k - 1))
+                publish(h, c, -s * (k - 1))
         if k == 1:
-            publish(0, c, 0)
-
-    def direct_far(c):
-        for way in (UP, DOWN):
-            send(1, c, 0, way, 1, 2 * sign(way))
-
-    def direct_near(c):
-        for way in (UP, DOWN):
-            send(1, c, 0, way, 0, sign(way))
-        publish(1, c, 0)
-
-    def forward(c):
-        for way in (UP, DOWN):
-            s = sign(way)
-            arrived(1, c, way, 1)
+            publish(h, c, 0)
+
+    def direct_far(h, c):
+        for way in (UP, DOWN):
+            send(h, c, 0, way, 1, 2 * sign(way))
+
+    def direct_near(h, c):
+        for way in (UP, DOWN):
+            send(h, c, 0, way, 0, sign(way))
+        publish(h, c, 0)
+
+    def forward(h, c):
+        for way in (UP, DOWN):
+            s = sign(way)
+            arrived(h, c, way, 1)
             if is_far(way, c):
-                send(1, c, -2 * s, way, 3, 2 * s)
-            send(1, c, -2 * s, way, 2, s)
-            publish(1, c, -2 * s)
-
-    def near(c):
-        for way in (UP, DOWN):
-            arrived(1, c, way, 0)
-            publish(1, c, -sign(way))
-
-    def collect(c):
-        for way in (UP, DOWN):
-            arrived(1, c, way, 2)
-            publish(1, c, -3 * sign(way))
+                send(h, c, -2 * s, way, 3, 2 * s)
+            send(h, c, -2 * s, way, 2, s)
+            publish(h, c, -2 * s)
+
+    def near(h, c):
+        for way in (UP, DOWN):
+            arrived(h, c, way, 0)
+            publish(h, c, -sign(way))
+
+    def collect(h, c):
+        for way in (UP, DOWN):
+            arrived(h, c, way, 2)
+            publish(h, c, -3 * sign(way))
         for way in (UP, DOWN):
             if is_far(way, c):
-                arrived(1, c, way, 3)
-                publish(1, c, -far * sign(way))
+                arrived(h, c, way, 3)
+                publish(h, c, -far * sign(way))
 
     def expert_half(h):
         with jax.named_scope(f"wwait{h}"):
@@ -360,32 +354,18 @@
             blk = jnp.dot(unperm, ypart[...], preferred_element_type=F32)
             gat_ref[:, h, me] = blk.reshape(rows, hs, width).astype(BF16)
 
-    expert_half(0)
-    ring(0, 1)
-    ring(1, 1)
-    expert_half(1)
-    direct_far(0)
-    direct_far(1)
-    comb(4)
-    ring(0, 2)
-    ring(1, 2)
-    direct_near(0)
-    direct_near(1)
-    comb(5)
-    forward(0)
-    forward(1)
-    ring(0, 3)
-    ring(1, 3)
-    comb(6)
-    near(0)
-    near(1)
-    comb(7)
-    ring(0, 4)
-    ring(1, 4)
-    collect(0)
-    collect(1)
-    ring(0, 5)
-    ring(1, 5)
+    events = {
+        "disp": disp, "bar": greet, "pair": lambda g: pair_copy(g).start(), "total": total, "hop": hop, "first": rs_first,
+        "relay": rs_relay, "zpair": lambda: zpair_copy().start(), "z": z_exchange, "comb": comb, "FIN": own_inputs,
+        "ffn": expert_half, "ring": ring, "dfar": direct_far, "dnear": direct_near, "fwd": forward, "near": near,
+        "coll": collect,
+    }
+    with jax.named_scope("x0"):
+        x_copies[0].wait()
+    with jax.named_scope("norm0"):
+        normalize_part(0, pl.ds(0, toks))
+    for event in ORDER:
+        events[event[0]](*event[1:])
 
     with jax.named_scope("end"):
         wait_bytes(gat_ref.at[:, :, pl.ds(0, chips)], pg_recv)
@@ -421,7 +401,9 @@
         own = slots // seq
         chips = seq // CORES
         groups = rows // GROUP_ROWS
-        ring_rows = RING_GROUPS * GROUP_ROWS
+        ring_groups = RS_PLAN.count("R")
+        ring_rows = ring_groups * GROUP_ROWS
+        hop_rows = max(ring_rows, 1)
         far = chips // 2
         hs = own // HALVES
         par = slots // CORES
@@ -448,18 +430,20 @@
                 pltpu.VMEM((rows, chips, own, width), BF16),
                 pltpu.VMEM((2, rows - ring_rows, own, width), BF16),
                 pltpu.VMEM((2, 4, rows - ring_rows, own, width), BF16),
-                pltpu.VMEM((2, far, ring_rows, own, width), BF16),
-                pltpu.VMEM((2, far + 1, ring_rows, own, width), BF16),
+                pltpu.VMEM((2, far, hop_rows, own, width), BF16),
+                pltpu.VMEM((2, far + 1, hop_rows, own, width), BF16),
                 pltpu.VMEM((CORES, par, 128), F32),
                 pltpu.VMEM((par, 128), F32),
                 pltpu.VMEM((chips, own, 128), BF16),
                 pltpu.VMEM((chips, own, 128), BF16),
                 pltpu.VMEM((count, width), BF16),
+                pltpu.VMEM((count, width), BF16),
                 pltpu.VMEM((experts, width, ff), BF16),
                 pltpu.VMEM((experts, ff, width), BF16),
                 pltpu.VMEM((count // HALVES, width), BF16),
-                dma((3,)), dma, dma((HALVES,)), dma, dma((groups,)), dma((2,)), dma((2,)),
-                dma((2, groups - RING_GROUPS)), dma((2, RING_GROUPS, far - 1)), dma, dma, dma,
+                pltpu.VMEM((2, slots, toks), BF16),
+                dma((4,)), dma, dma((HALVES,)), dma, dma((groups,)), dma((2,)), dma((2,)),
+                dma((2, groups - ring_groups)), dma((2, max(ring_groups, 1), far - 1)), dma, dma, dma,
                 dma((HALVES, CHUNKS, 2, 4)), dma, dma,
             ],
             compiler_params=pltpu.CompilerParams(

time: 51 us -> 48.6 us (0.953)
  Pallas kernels: 50.1 us -> 47.6 us
    pallas_call x1, Pallas kernels: 46.2 us -> 43.8 us  [shard_body(): pl.pallas_call(functools.partial(_exchange_kernel, dims), out_shape=(pltp...]
where the time goes in v4:
time: 48.6 us; the launch traced here: 48.5 us
  Pallas kernels  47.6 us (98%)
  between operations  0.84 us (2%)
    pallas_call x1, Pallas kernels, shard_body(): pl.pallas_call(functools.partial(_exchange_kernel, dims), out_shape=(pltp...  43.8 us
    pallas_call x1, Pallas kernels, shard_body(): pl.pallas_call(_combine_kernel, out_shape=jax.ShapeDtypeStruct((rows, tok...  3.84 us

profile of v4, /device:TPU:21, one launch (start us, length us, event | category | flops | bytes accessed | tf_op | source)
XLA Modules:
  0.0 48.5 jit_solution(17347531439884914745)
XLA Ops:
  0.7 0.0 copy-start
  0.7 43.8 %exchange.1 = (bf16[8,1024,256]{2,1,0:T(8,128)(2,1)S(1)}, bf16[8,2,16,8,384]{4,3,2,1,0:T(8,128)(2,1)S(1)}) custom-call(s32[8]{0:T(128)} %len_ref.3, f32[1]{0:T(128)S(6)} %copy.7.scale_ref, bf16[384,256]{1,0:T(8,128)(2,1)} %phi_ref.1, bf16[8,1024,384]{2,1,0:T(8,128)(2,1)} %tok_ref.1, bf16[8,384,1536]{2,1,0:T(8,128)(2,1)} %win_ref.1, ...), custom_call_target="tpu_custom_call" | custom-call | tf_op jit(solution)/shard_map/exchange/pallas_call | solution.py:416
  44.5 0.0 copy-done
  44.5 3.8 %combine.1 = bf16[8,1024,384]{2,1,0:T(8,128)(2,1)} custom-call(s32[8]{0:T(128)S(1)} %copy-done, bf16[8,1024,256]{2,1,0:T(8,128)(2,1)S(1)} %get-tuple-element.7.comb_ref, bf16[8,256,384]{2,1,0:T(8,128)(2,1)S(1)} %bitcast.1), custom_call_target="tpu_custom_call" | custom-call | tf_op jit(solution)/shard_map/combine/pallas_call | solution.py:454
Async XLA Ops:
  0.7 43.8 %copy-start = (s32[8]{0:T(128)S(1)}, s32[8]{0:T(128)}, u32[]{:S(2)}) copy-start(s32[8]{0:T(128)} %len_ref.3) | copy-start | bytes 100

commit v5 on v4

--- a/solution.py
+++ b/solution.py
@@ -16,17 +16,17 @@
 HALVES = 2
 CORES = 2
 CHUNKS = 2
-RS_PLAN = "TTTT"
 ORDER = (
-    ("disp", 0), ("disp", 1), ("bar",), ("disp", 2), ("pair", 0), ("disp", 3), ("disp", 4), ("pair", 1),
-    ("total", 0), ("first", 0), ("disp", 5), ("disp", 6), ("pair", 2), ("total", 1), ("first", 1), ("disp", 7),
-    ("disp", 8), ("total", 2), ("first", 2), ("pair", 3), ("total", 3), ("zpair",), ("first", 3), ("relay", 0),
-    ("z",), ("comb", 0), ("comb", 1), ("comb", 2), ("relay", 2), ("relay", 1), ("comb", 3), ("relay", 3),
-    ("comb", 4), ("comb", 5), ("FIN",), ("ffn", 0), ("ring", 0, 0, 1), ("dnear", 0, 1), ("dfar", 0, 1),
-    ("ffn", 1), ("dfar", 1, 1), ("ring", 0, 0, 2), ("dfar", 1, 0), ("dnear", 1, 1), ("comb", 6),
-    ("dnear", 1, 0), ("near", 0, 1), ("comb", 7), ("ring", 0, 0, 3), ("fwd", 1, 1), ("fwd", 0, 1),
-    ("near", 1, 1), ("fwd", 1, 0), ("near", 1, 0), ("ring", 0, 0, 4), ("coll", 1, 1), ("coll", 0, 1),
-    ("ring", 0, 0, 5), ("coll", 1, 0),
+    ("disp", 0), ("disp", 1), ("disp", 2), ("bar",), ("pair", 0), ("disp", 3), ("disp", 4), ("total", 0),
+    ("first", 0, 0), ("first", 0, 1), ("pair", 1), ("disp", 5), ("total", 1), ("first", 1, 0), ("disp", 6),
+    ("first", 1, 1), ("pair", 2), ("disp", 7), ("disp", 8), ("relay", 0, 0), ("pair", 3), ("zpair",),
+    ("total", 2), ("first", 2, 0), ("comb", 0), ("first", 2, 1), ("total", 3), ("first", 3, 0), ("z",),
+    ("first", 3, 1), ("relay", 1, 0), ("comb", 1), ("comb", 2), ("relay", 2, 0), ("comb", 3), ("relay", 3, 0),
+    ("comb", 4), ("comb", 5), ("relay", 0, 1), ("relay", 1, 1), ("relay", 2, 1), ("relay", 3, 1), ("comb", 6),
+    ("fin", 0), ("ffn", 0), ("dfar", 0, 0), ("dfar", 0, 1), ("dnear", 0, 1), ("dnear", 0, 0), ("fin", 1),
+    ("ffn", 1), ("dfar", 1, 0), ("comb", 7), ("dfar", 1, 1), ("fwd", 0, 1), ("fwd", 0, 0), ("near", 0, 0),
+    ("fwd", 1, 0), ("near", 0, 1), ("dnear", 1, 0), ("fwd", 1, 1), ("dnear", 1, 1), ("coll", 1, 0),
+    ("coll", 0, 0), ("near", 1, 0), ("coll", 0, 1), ("near", 1, 1), ("coll", 1, 1),
 )
 PARTS = 1
 VMEM_LIMIT = 52 * 1024 * 1024
@@ -34,9 +34,9 @@
 
 
 def _exchange_kernel(dims, len_ref, scale_ref, phi_ref, tok_ref, win_ref, wout_ref, comb_ref, gat_ref,
-                     xbuf, xnbuf, phi_in, phi_ring, phi_comb, part, pin, chip, cbuf, rbuf, hsend, hrecv, zpart, zpin, zchip, zrecv,
+                     xbuf, xnbuf, phi_in, phi_ring, phi_comb, part, pin, chip, cbuf, rbuf, zpart, zpin, zchip, zrecv,
                      slot_in, by_expert, win, wout, ypart, wbuf,
-                     x_sem, phi_sem, w_sem, pr_send, pr_recv, zp_sem, z_sem, relay_recv, hop_recv, fin_recv, hfin_recv, rs_send,
+                     x_sem, phi_sem, w_sem, pr_send, pr_recv, zp_sem, z_sem, relay_recv, fin_recv, rs_send,
                      ag_recv, ag_send, pg_recv):
     rows, toks, width, slots, seq, experts = dims
     chips = seq // CORES
@@ -45,7 +45,6 @@
     groups = rows // GROUP_ROWS
     far = chips // 2
     half_e = experts // HALVES
-    ring_groups = RS_PLAN.count("R")
     hs = own // HALVES
     par = slots // CORES
 
@@ -85,7 +84,7 @@
 
     n0 = lax.broadcasted_iota(jnp.int32, (slots, slots), 0)
     n1 = lax.broadcasted_iota(jnp.int32, (slots, slots), 1)
-    ring_src = ((n0 % par) // own * CORES + n0 // par) * own + n0 % own
+    ring_src = ((n0 % (par // HALVES)) // hs * CORES + n0 // par) * own + (n0 % par) // (par // HALVES) * hs + n0 % hs
     comb_src = (n0 % (seq * hs)) // hs * own + n0 // (seq * hs) * hs + n0 % hs
     ring_hot = jnp.where(n1 == ring_src, 1.0, 0.0).astype(BF16)
     comb_hot = jnp.where(n1 == comb_src, 1.0, 0.0).astype(BF16)
@@ -121,7 +120,7 @@
                 if lo < hi:
                     s = jnp.dot(wbuf[(r - 1) % 2], xbuf[r - 1, :, lo:hi], preferred_element_type=F32).astype(BF16)
                     for p in range(CORES):
-                        part[p, r - 1, :, :, lo:hi] = s[p * par:(p + 1) * par].reshape(chips, own, hi - lo)
+                        part[p, r - 1, :, :, :, lo:hi] = s[p * par:(p + 1) * par].reshape(HALVES, chips, hs, hi - lo)
             if r + 1 < rows:
                 normalize_part(r + 1, ts)
             if r < rows:
@@ -160,48 +159,28 @@
     def last_of(way, index):
         return far if is_far(way, index) else far - 1
 
-    def hop(g, step):
+    def rs_first(g, h):
         for way in (UP, DOWN):
             s = sign(way)
-            k = last_of(way, g) - step
-            if k < 1:
-                continue
-            if step == 0:
-                src = chip.at[span(g), chip_at(s * k)]
-            else:
-                with jax.named_scope(f"hop{g}_{step}_{way}"):
-                    wait_bytes(hrecv.at[way, k + 1, span(g)], hop_recv.at[way, g, k - 1])
-                total = chip[span(g), chip_at(s * k)].astype(F32) + hrecv[way, k + 1, span(g)].astype(F32)
-                hsend[way, k, span(g)] = total.astype(BF16)
-                src = hsend.at[way, k, span(g)]
-            recv = hfin_recv if k == 1 else hop_recv.at[way, g, k - 2]
-            remote(src, hrecv.at[way, k, span(g)], rs_send, recv, dev_at(s)).start()
-
-    def late(g):
-        return pl.ds((g - ring_groups) * GROUP_ROWS, GROUP_ROWS)
-
-    def rs_first(g):
+            relay = relay_recv.at[way, g, h]
+            if is_far(way, g + h):
+                remote(chip.at[span(g), h, chip_at(far * s)], rbuf.at[way, 0, h, span(g)], rs_send, relay, dev_at(2 * s)).start()
+            remote(chip.at[span(g), h, chip_at(3 * s)], rbuf.at[way, 1, h, span(g)], rs_send, relay, dev_at(s)).start()
         for way in (UP, DOWN):
             s = sign(way)
-            relay = relay_recv.at[way, g - ring_groups]
-            if is_far(way, g):
-                remote(chip.at[span(g), chip_at(far * s)], rbuf.at[way, 0, late(g)], rs_send, relay, dev_at(2 * s)).start()
-            remote(chip.at[span(g), chip_at(3 * s)], rbuf.at[way, 1, late(g)], rs_send, relay, dev_at(s)).start()
+            remote(chip.at[span(g), h, chip_at(s)], rbuf.at[way, 3, h, span(g)], rs_send, fin_recv.at[h], dev_at(s)).start()
+
+    def rs_relay(g, h):
         for way in (UP, DOWN):
             s = sign(way)
-            remote(chip.at[span(g), chip_at(s)], rbuf.at[way, 3, late(g)], rs_send, fin_recv, dev_at(s)).start()
-
-    def rs_relay(g):
-        for way in (UP, DOWN):
-            s = sign(way)
-            first = 0 if is_far(way, g) else 1
-            with jax.named_scope(f"relay{g}_{way}"):
-                wait_bytes(rbuf.at[way, pl.ds(first, 2 - first), late(g)], relay_recv.at[way, g - ring_groups])
-            total = chip[span(g), chip_at(2 * s)].astype(F32)
+            first = 0 if is_far(way, g + h) else 1
+            with jax.named_scope(f"relay{g}_{h}_{way}"):
+                wait_bytes(rbuf.at[way, pl.ds(first, 2 - first), h, span(g)], relay_recv.at[way, g, h])
+            total = chip[span(g), h, chip_at(2 * s)].astype(F32)
             for kind in range(first, 2):
-                total = total + rbuf[way, kind, late(g)].astype(F32)
-            cbuf[way, late(g)] = total.astype(BF16)
-            remote(cbuf.at[way, late(g)], rbuf.at[way, 2, late(g)], rs_send, fin_recv, dev_at(2 * s)).start()
+                total = total + rbuf[way, kind, h, span(g)].astype(F32)
+            cbuf[way, h, span(g)] = total.astype(BF16)
+            remote(cbuf.at[way, h, span(g)], rbuf.at[way, 2, h, span(g)], rs_send, fin_recv.at[h], dev_at(2 * s)).start()
 
     def z_exchange():
         zpair_copy().wait_recv()
@@ -215,7 +194,7 @@
         split = split + jnp.where((zl >= 2 * rows) & (zl < 3 * rows), pltpu.roll(low, 2 * rows, 1), 0.0)
         zchip[...] = split.astype(BF16).reshape(zchip.shape)
         for delta in range(1, chips):
-            remote(zchip.at[chip_at(delta)], zrecv.at[delta], z_sem.at[0], z_sem.at[1], dev_at(delta)).start()
+            remote(zchip.at[:, chip_at(delta)], zrecv.at[delta], z_sem.at[0], z_sem.at[1], dev_at(delta)).start()
 
     def weights(h):
         es = pl.ds(h * half_e, half_e)
@@ -245,42 +224,34 @@
         with jax.named_scope("barrier"):
             pl.semaphore_wait(barrier, chips)
 
-    count = rows * own
-    i0 = lax.broadcasted_iota(jnp.int32, (count, count), 0)
-    i1 = lax.broadcasted_iota(jnp.int32, (count, count), 1)
     rb = rows * per
-    src = ((i0 % rb) // per) * own + (i0 // rb) * per + i0 % per
-    perm = jnp.where(i1 == src, 1.0, 0.0).astype(BF16)
     hc = half_e * rb
     j0 = lax.broadcasted_iota(jnp.int32, (hc, hc), 0)
     j1 = lax.broadcasted_iota(jnp.int32, (hc, hc), 1)
     back = ((j0 % hs) // per) * rb + (j0 // hs) * per + j0 % per
     unperm = jnp.where(j1 == back, 1.0, 0.0).astype(BF16)
-
-    def own_inputs():
-        with jax.named_scope("zwait"):
-            wait_bytes(zrecv.at[pl.ds(1, chips - 1)], z_sem.at[1])
-        zsum = zchip[z].astype(F32)
+    src = ((j0 % rb) // per) * hs + (j0 // rb) * per + j0 % per
+    perm = jnp.where(j1 == src, 1.0, 0.0).astype(BF16)
+
+    def own_inputs(h):
+        if h == 0:
+            with jax.named_scope("zwait"):
+                wait_bytes(zrecv.at[pl.ds(1, chips - 1)], z_sem.at[1])
+        zsum = zchip[h, z].astype(F32)
         for delta in range(1, chips):
-            zsum = zsum + zrecv[delta].astype(F32)
+            zsum = zsum + zrecv[delta, h].astype(F32)
         lane = lax.broadcasted_iota(jnp.int32, zsum.shape, 1)
-        if ring_groups:
-            with jax.named_scope("hfin"):
-                wait_bytes(hrecv.at[:, 1], hfin_recv)
-        with jax.named_scope("fin"):
-            wait_bytes(rbuf.at[:, pl.ds(2, 2)], fin_recv)
+        with jax.named_scope(f"fin{h}"):
+            wait_bytes(rbuf.at[:, pl.ds(2, 2), h], fin_recv.at[h])
         for b in range(rows):
-            s = chip[b, z].astype(F32)
+            s = chip[b, h, z].astype(F32)
             for way in (UP, DOWN):
-                if b < ring_groups * GROUP_ROWS:
-                    s = s + hrecv[way, 1, b].astype(F32)
-                else:
-                    lb = b - ring_groups * GROUP_ROWS
-                    s = s + (rbuf[way, 2, lb].astype(F32) + rbuf[way, 3, lb].astype(F32))
+                s = s + (rbuf[way, 2, h, b].astype(F32) + rbuf[way, 3, h, b].astype(F32))
             mine = (lane % rows == b) & (lane < 3 * rows)
             zb = jnp.sum(jnp.where(mine, zsum, 0.0), axis=-1, keepdims=True)
-            slot_in[b * own:(b + 1) * own] = (s / zb).astype(BF16)
-        by_expert[...] = jnp.dot(perm, slot_in[...], preferred_element_type=F32).astype(BF16)
+            slot_in[h, b] = s / zb
+        inputs = slot_in[h].reshape(rows * hs, width).astype(BF16)
+        by_expert[h] = jnp.dot(perm, inputs, preferred_element_type=F32).astype(BF16)
 
     crows = rows // CHUNKS
 
@@ -348,15 +319,15 @@
         with jax.named_scope(f"ffn{h}"):
             for i in range(half_e):
                 e = h * half_e + i
-                hid = jnp.dot(by_expert[e * rb:(e + 1) * rb], win[e], preferred_element_type=F32)
+                hid = jnp.dot(by_expert[h, i * rb:(i + 1) * rb], win[e], preferred_element_type=F32)
                 hid = jax.nn.gelu(hid).astype(BF16)
                 ypart[i * rb:(i + 1) * rb] = jnp.dot(hid, wout[e], preferred_element_type=F32).astype(BF16)
             blk = jnp.dot(unperm, ypart[...], preferred_element_type=F32)
             gat_ref[:, h, me] = blk.reshape(rows, hs, width).astype(BF16)
 
     events = {
-        "disp": disp, "bar": greet, "pair": lambda g: pair_copy(g).start(), "total": total, "hop": hop, "first": rs_first,
-        "relay": rs_relay, "zpair": lambda: zpair_copy().start(), "z": z_exchange, "comb": comb, "FIN": own_inputs,
+        "disp": disp, "bar": greet, "pair": lambda g: pair_copy(g).start(), "total": total, "first": rs_first,
+        "relay": rs_relay, "zpair": lambda: zpair_copy().start(), "z": z_exchange, "comb": comb, "fin": own_inputs,
         "ffn": expert_half, "ring": ring, "dfar": direct_far, "dnear": direct_near, "fwd": forward, "near": near,
         "coll": collect,
     }
@@ -373,7 +344,7 @@
         wait_bytes(pin, pr_send)
         zpair_copy().wait_send()
         wait_bytes(zrecv.at[pl.ds(1, chips - 1)], z_sem.at[0])
-        wait_bytes(part.at[0, :, pl.ds(0, chips - 1)], rs_send)
+        wait_bytes(part.at[0, :, :, pl.ds(0, chips - 1)], rs_send)
 
 
 def _combine_kernel(len_ref, comb_ref, gat_ref, out_ref, ybuf, y_sem):
@@ -401,9 +372,6 @@
         own = slots // seq
         chips = seq // CORES
         groups = rows // GROUP_ROWS
-        ring_groups = RS_PLAN.count("R")
-        ring_rows = ring_groups * GROUP_ROWS
-        hop_rows = max(ring_rows, 1)
         far = chips // 2
         hs = own // HALVES
         par = slots // CORES
@@ -425,25 +393,23 @@
                 pltpu.VMEM((width, slots), BF16),
                 pltpu.VMEM((slots, width), BF16),
                 pltpu.VMEM((slots, width), BF16),
-                pltpu.VMEM((CORES, rows, chips, own, width), BF16),
-                pltpu.VMEM((rows, chips, own, width), BF16),
-                pltpu.VMEM((rows, chips, own, width), BF16),
-                pltpu.VMEM((2, rows - ring_rows, own, width), BF16),
-                pltpu.VMEM((2, 4, rows - ring_rows, own, width), BF16),
-                pltpu.VMEM((2, far, hop_rows, own, width), BF16),
-                pltpu.VMEM((2, far + 1, hop_rows, own, width), BF16),
+                pltpu.VMEM((CORES, rows, HALVES, chips, hs, width), BF16),
+                pltpu.VMEM((rows, HALVES, chips, hs, width), BF16),
+                pltpu.VMEM((rows, HALVES, chips, hs, width), BF16),
+                pltpu.VMEM((2, HALVES, rows, hs, width), BF16),
+                pltpu.VMEM((2, 4, HALVES, rows, hs, width), BF16),
                 pltpu.VMEM((CORES, par, 128), F32),
                 pltpu.VMEM((par, 128), F32),
-                pltpu.VMEM((chips, own, 128), BF16),
-                pltpu.VMEM((chips, own, 128), BF16),
-                pltpu.VMEM((count, width), BF16),
-                pltpu.VMEM((count, width), BF16),
+                pltpu.VMEM((HALVES, chips, hs, 128), BF16),
+                pltpu.VMEM((chips, HALVES, hs, 128), BF16),
+                pltpu.VMEM((HALVES, rows, hs, width), F32),
+                pltpu.VMEM((HALVES, count // HALVES, width), BF16),
                 pltpu.VMEM((experts, width, ff), BF16),
                 pltpu.VMEM((experts, ff, width), BF16),
                 pltpu.VMEM((count // HALVES, width), BF16),
                 pltpu.VMEM((2, slots, toks), BF16),
                 dma((4,)), dma, dma((HALVES,)), dma, dma((groups,)), dma((2,)), dma((2,)),
-                dma((2, groups - ring_groups)), dma((2, max(ring_groups, 1), far - 1)), dma, dma, dma,
+                dma((2, groups, HALVES)), dma((HALVES,)), dma,
                 dma((HALVES, CHUNKS, 2, 4)), dma, dma,
             ],
             compiler_params=pltpu.CompilerParams(

time: 48.6 us -> 47.4 us (0.975)
  Pallas kernels: 47.6 us -> 46.5 us
    pallas_call x1, Pallas kernels: 43.8 us -> 42.6 us  [shard_body(): pl.pallas_call(functools.partial(_exchange_kernel, dims), out_shape=(pltp...]
where the time goes in v5:
time: 47.4 us; the launch traced here: 47.3 us
  Pallas kernels  46.5 us (98%)
  between operations  0.84 us (2%)
    pallas_call x1, Pallas kernels, shard_body(): pl.pallas_call(functools.partial(_exchange_kernel, dims), out_shape=(pltp...  42.6 us
    pallas_call x1, Pallas kernels, shard_body(): pl.pallas_call(_combine_kernel, out_shape=jax.ShapeDtypeStruct((rows, tok...  3.84 us

profile of v5, /device:TPU:21, one launch (start us, length us, event | category | flops | bytes accessed | tf_op | source)
XLA Modules:
  0.0 47.3 jit_solution(12784354095861284190)
XLA Ops:
  0.7 0.0 copy-start
  0.7 42.6 %exchange.1 = (bf16[8,1024,256]{2,1,0:T(8,128)(2,1)S(1)}, bf16[8,2,16,8,384]{4,3,2,1,0:T(8,128)(2,1)S(1)}) custom-call(s32[8]{0:T(128)} %len_ref.3, f32[1]{0:T(128)S(6)} %copy.7.scale_ref, bf16[384,256]{1,0:T(8,128)(2,1)} %phi_ref.1, bf16[8,1024,384]{2,1,0:T(8,128)(2,1)} %tok_ref.1, bf16[8,384,1536]{2,1,0:T(8,128)(2,1)} %win_ref.1, ...), custom_call_target="tpu_custom_call" | custom-call | tf_op jit(solution)/shard_map/exchange/pallas_call | solution.py:384
  43.3 0.0 copy-done
  43.3 3.8 %combine.1 = bf16[8,1024,384]{2,1,0:T(8,128)(2,1)} custom-call(s32[8]{0:T(128)S(1)} %copy-done, bf16[8,1024,256]{2,1,0:T(8,128)(2,1)S(1)} %get-tuple-element.7.comb_ref, bf16[8,256,384]{2,1,0:T(8,128)(2,1)S(1)} %bitcast.1), custom_call_target="tpu_custom_call" | custom-call | tf_op jit(solution)/shard_map/combine/pallas_call | solution.py:420
Async XLA Ops:
  0.7 42.6 %copy-start = (s32[8]{0:T(128)S(1)}, s32[8]{0:T(128)}, u32[]{:S(2)}) copy-start(s32[8]{0:T(128)} %len_ref.3) | copy-start | bytes 100

commit v6 on v5

--- a/solution.py
+++ b/solution.py
@@ -18,25 +18,25 @@
 CHUNKS = 2
 ORDER = (
     ("disp", 0), ("disp", 1), ("disp", 2), ("bar",), ("pair", 0), ("disp", 3), ("disp", 4), ("total", 0),
-    ("first", 0, 0), ("first", 0, 1), ("pair", 1), ("disp", 5), ("total", 1), ("first", 1, 0), ("disp", 6),
-    ("first", 1, 1), ("pair", 2), ("disp", 7), ("disp", 8), ("relay", 0, 0), ("pair", 3), ("zpair",),
-    ("total", 2), ("first", 2, 0), ("comb", 0), ("first", 2, 1), ("total", 3), ("first", 3, 0), ("z",),
-    ("first", 3, 1), ("relay", 1, 0), ("comb", 1), ("comb", 2), ("relay", 2, 0), ("comb", 3), ("relay", 3, 0),
-    ("comb", 4), ("comb", 5), ("relay", 0, 1), ("relay", 1, 1), ("relay", 2, 1), ("relay", 3, 1), ("comb", 6),
-    ("fin", 0), ("ffn", 0), ("dfar", 0, 0), ("dfar", 0, 1), ("dnear", 0, 1), ("dnear", 0, 0), ("fin", 1),
-    ("ffn", 1), ("dfar", 1, 0), ("comb", 7), ("dfar", 1, 1), ("fwd", 0, 1), ("fwd", 0, 0), ("near", 0, 0),
-    ("fwd", 1, 0), ("near", 0, 1), ("dnear", 1, 0), ("fwd", 1, 1), ("dnear", 1, 1), ("coll", 1, 0),
-    ("coll", 0, 0), ("near", 1, 0), ("coll", 0, 1), ("near", 1, 1), ("coll", 1, 1),
+    ("pair", 1), ("first", 0, 0), ("disp", 5), ("first", 0, 1), ("disp", 6), ("total", 1), ("first", 1, 1),
+    ("pair", 2), ("first", 1, 0), ("disp", 7), ("disp", 8), ("total", 2), ("pair", 3), ("zpair",),
+    ("first", 2, 0), ("relay", 0, 0), ("comb", 0), ("total", 3), ("first", 3, 0), ("first", 3, 1), ("z",),
+    ("first", 2, 1), ("comb", 1), ("relay", 1, 0), ("comb", 2), ("relay", 2, 0), ("comb", 3), ("relay", 3, 0),
+    ("comb", 4), ("comb", 5), ("relay", 0, 1), ("comb", 6), ("relay", 1, 1), ("relay", 2, 1), ("relay", 3, 1),
+    ("fin", 0), ("ffn", 0), ("dfar", 0, 0), ("dfar", 0, 1), ("dnear", 0, 1), ("fin", 1), ("dnear", 0, 0),
+    ("ffn", 1), ("dfar", 1, 0), ("dfar", 1, 1), ("near", 0, 0), ("fwd", 0, 0), ("fwd", 0, 1), ("near", 0, 1),
+    ("fwd", 1, 0), ("dnear", 1, 1), ("fwd", 1, 1), ("dnear", 1, 0), ("coll", 0, 0), ("comb", 7),
+    ("coll", 1, 0), ("near", 1, 1), ("coll", 0, 1), ("coll", 1, 1), ("near", 1, 0),
 )
-PARTS = 1
+PARTS = 2
 VMEM_LIMIT = 52 * 1024 * 1024
 COMBINE_LIMIT = 20 * 1024 * 1024
 
 
-def _exchange_kernel(dims, len_ref, scale_ref, phi_ref, tok_ref, win_ref, wout_ref, comb_ref, gat_ref,
-                     xbuf, xnbuf, phi_in, phi_ring, phi_comb, part, pin, chip, cbuf, rbuf, zpart, zpin, zchip, zrecv,
+def _exchange_kernel(dims, len_hbm, scale_ref, phi_ref, tok_ref, win_ref, wout_ref, comb_ref, gat_ref, lens_ref,
+                     len_ref, xbuf, xnbuf, phi_in, phi_ring, phi_comb, part, pin, chip, cbuf, rbuf, zpart, zpin, zchip, zrecv,
                      slot_in, by_expert, win, wout, ypart, wbuf,
-                     x_sem, phi_sem, w_sem, pr_send, pr_recv, zp_sem, z_sem, relay_recv, fin_recv, rs_send,
+                     x_sem, phi_sem, scalar_sem, w_sem, pr_send, pr_recv, zp_sem, z_sem, relay_recv, fin_recv, rs_send,
                      ag_recv, ag_send, pg_recv):
     rows, toks, width, slots, seq, experts = dims
     chips = seq // CORES
@@ -73,7 +73,9 @@
     x_parts = {0: pl.ds(0, 1), 1: pl.ds(1, 1), 2: pl.ds(2, 2), 4: pl.ds(4, rows - 4)}
     x_copies = {b: pltpu.make_async_copy(tok_ref.at[p], xbuf.at[p], x_sem.at[i]) for i, (b, p) in enumerate(x_parts.items())}
     phi_copy = pltpu.make_async_copy(phi_ref, phi_in, phi_sem)
+    len_copy = pltpu.make_async_copy(len_hbm, len_ref, scalar_sem)
     phi_copy.start()
+    len_copy.start()
     x_copies[0].start()
     x_copies[1].start()
 
@@ -88,9 +90,10 @@
     comb_src = (n0 % (seq * hs)) // hs * own + n0 // (seq * hs) * hs + n0 % hs
     ring_hot = jnp.where(n1 == ring_src, 1.0, 0.0).astype(BF16)
     comb_hot = jnp.where(n1 == comb_src, 1.0, 0.0).astype(BF16)
-    gain = scale_ref[0]
     with jax.named_scope("phiwait"):
         phi_copy.wait()
+        len_copy.wait()
+    gain = scale_ref[0]
     x_copies[2].start()
     x_copies[4].start()
     params = phi_in[...].astype(F32)
@@ -101,34 +104,40 @@
     bound = gain * 1.01
     zlane = lax.broadcasted_iota(jnp.int32, (slots, 128), 1)
     zpart[...] = jnp.zeros_like(zpart)
+    row_id = lax.broadcasted_iota(jnp.int32, lens_ref.shape, 0)
+    lens = jnp.zeros(lens_ref.shape, jnp.int32)
+    for b in range(rows):
+        lens = jnp.where(row_id == b, len_ref[b], lens)
+    lens_ref[...] = lens
 
     def normalize_part(b, ts):
         xf = xbuf[b, ts].astype(F32)
         inv = lax.rsqrt(jnp.sum(xf * xf, axis=-1, keepdims=True) + 1e-6)
         xnbuf[b, ts] = (xf * inv).astype(BF16)
 
+    def weigh(r, ts):
+        lt = lax.dot_general(phi_ring[...], xnbuf[r, ts], NT, preferred_element_type=F32)
+        pos = me * toks + ts.start + lax.broadcasted_iota(jnp.int32, (1, ts.size), 1)
+        w = jnp.exp(lt - jnp.where(pos < len_ref[r], bound, 1e30))
+        wbuf[r % 2, :, ts] = w.astype(BF16)
+        return sum(w[:, i * 128:(i + 1) * 128] for i in range(ts.size // 128))
+
+    def slot_sums(r, lo, hi):
+        s = jnp.dot(wbuf[r % 2], xbuf[r, :, lo:hi], preferred_element_type=F32).astype(BF16)
+        for p in range(CORES):
+            part[p, r, :, :, :, lo:hi] = s[p * par:(p + 1) * par].reshape(HALVES, chips, hs, hi - lo)
+
     def dispatch_stage(r):
         tile = toks // PARTS
         zs = jnp.zeros((slots, 128), F32)
-        cut = -(-width // (256 * PARTS)) * 256
+        if r >= 1:
+            slot_sums(r - 1, 0, width)
         for c in range(PARTS):
             ts = pl.ds(c * tile, tile)
             if r < rows:
-                lt = lax.dot_general(phi_ring[...], xnbuf[r, ts], NT, preferred_element_type=F32)
-            if r >= 1:
-                lo, hi = min(c * cut, width), min((c + 1) * cut, width)
-                if lo < hi:
-                    s = jnp.dot(wbuf[(r - 1) % 2], xbuf[r - 1, :, lo:hi], preferred_element_type=F32).astype(BF16)
-                    for p in range(CORES):
-                        part[p, r - 1, :, :, :, lo:hi] = s[p * par:(p + 1) * par].reshape(HALVES, chips, hs, hi - lo)
+                zs = zs + weigh(r, ts)
             if r + 1 < rows:
                 normalize_part(r + 1, ts)
-            if r < rows:
-                pos = me * toks + c * tile + lax.broadcasted_iota(jnp.int32, (1, tile), 1)
-                w = jnp.exp(lt - jnp.where(pos < len_ref[r], bound, 1e30))
-                for i in range(tile // 128):
-                    zs = zs + w[:, i * 128:(i + 1) * 128]
-                wbuf[r % 2, :, ts] = w.astype(BF16)
         if r < rows:
             zsum = jnp.sum(zs, axis=1, keepdims=True)
             hit = jnp.where(zlane == r, zsum, zpart[...].reshape(slots, 128))
@@ -155,9 +164,6 @@
 
     def is_far(way, index):
         return (index % 2 == 0) == (way == UP)
-
-    def last_of(way, index):
-        return far if is_far(way, index) else far - 1
 
     def rs_first(g, h):
         for way in (UP, DOWN):
@@ -255,39 +261,28 @@
 
     crows = rows // CHUNKS
 
-    def block(h, c, delta):
-        return gat_ref.at[pl.ds(c * crows, crows), h, dev_at(delta)]
-
-    def send(h, c, delta, way, kind, to):
-        remote(block(h, c, delta), block(h, c, delta), ag_send, ag_recv.at[h, c, way, kind], dev_at(to)).start()
-
-    def arrived(h, c, way, kind):
-        with jax.named_scope(f"ag_h{h}_c{c}_w{way}_k{kind}"):
-            wait_bytes(block(h, c, 0), ag_recv.at[h, c, way, kind])
+    def chunk(c):
+        return pl.ds(c * crows, crows)
+
+    def send(h, c, delta, sem, to):
+        ref = gat_ref.at[chunk(c), h, dev_at(delta)]
+        remote(ref, ref, ag_send, ag_recv.at[h, c, sem], dev_at(to)).start()
+
+    def arrived(h, c, sem, count):
+        with jax.named_scope(f"ag_h{h}_c{c}_s{sem}"):
+            wait_bytes(gat_ref.at[chunk(c), h, pl.ds(0, count)], ag_recv.at[h, c, sem])
 
     def publish(h, c, delta):
-        remote(block(h, c, delta), block(h, c, delta), ag_send, pg_recv, partner).start()
-
-    def ring(h, c, k):
-        for way in (UP, DOWN):
-            s = sign(way)
-            last = last_of(way, c)
-            if k > 1 and k - 1 <= last:
-                arrived(h, c, way, k - 2)
-            if k <= last:
-                send(h, c, -s * (k - 1), way, k - 1, s)
-            if k > 1 and k - 1 <= last:
-                publish(h, c, -s * (k - 1))
-        if k == 1:
-            publish(h, c, 0)
+        ref = gat_ref.at[chunk(c), h, dev_at(delta)]
+        remote(ref, ref, ag_send, pg_recv.at[c], partner).start()
 
     def direct_far(h, c):
         for way in (UP, DOWN):
-            send(h, c, 0, way, 1, 2 * sign(way))
+            send(h, c, 0, way, 2 * sign(way))
 
     def direct_near(h, c):
         for way in (UP, DOWN):
-            send(h, c, 0, way, 0, sign(way))
+            send(h, c, 0, 2, sign(way))
         publish(h, c, 0)
 
     def forward(h, c):
@@ -295,23 +290,20 @@
             s = sign(way)
             arrived(h, c, way, 1)
             if is_far(way, c):
-                send(h, c, -2 * s, way, 3, 2 * s)
-            send(h, c, -2 * s, way, 2, s)
+                send(h, c, -2 * s, 3, 2 * s)
+            send(h, c, -2 * s, 3, s)
             publish(h, c, -2 * s)
 
     def near(h, c):
-        for way in (UP, DOWN):
-            arrived(h, c, way, 0)
-            publish(h, c, -sign(way))
+        arrived(h, c, 2, 2)
+        publish(h, c, -1)
+        publish(h, c, 1)
 
     def collect(h, c):
-        for way in (UP, DOWN):
-            arrived(h, c, way, 2)
-            publish(h, c, -3 * sign(way))
-        for way in (UP, DOWN):
-            if is_far(way, c):
-                arrived(h, c, way, 3)
-                publish(h, c, -far * sign(way))
+        arrived(h, c, 3, 3)
+        publish(h, c, -3)
+        publish(h, c, 3)
+        publish(h, c, -far if is_far(UP, c) else far)
 
     def expert_half(h):
         with jax.named_scope(f"wwait{h}"):
@@ -328,7 +320,7 @@
     events = {
         "disp": disp, "bar": greet, "pair": lambda g: pair_copy(g).start(), "total": total, "first": rs_first,
         "relay": rs_relay, "zpair": lambda: zpair_copy().start(), "z": z_exchange, "comb": comb, "fin": own_inputs,
-        "ffn": expert_half, "ring": ring, "dfar": direct_far, "dnear": direct_near, "fwd": forward, "near": near,
+        "ffn": expert_half, "dfar": direct_far, "dnear": direct_near, "fwd": forward, "near": near,
         "coll": collect,
     }
     with jax.named_scope("x0"):
@@ -339,7 +331,8 @@
         events[event[0]](*event[1:])
 
     with jax.named_scope("end"):
-        wait_bytes(gat_ref.at[:, :, pl.ds(0, chips)], pg_recv)
+        for c in range(CHUNKS):
+            wait_bytes(gat_ref.at[chunk(c), :, pl.ds(0, chips)], pg_recv.at[c])
         wait_bytes(gat_ref.at[:, :, pl.ds(0, seq - 1)], ag_send)
         wait_bytes(pin, pr_send)
         zpair_copy().wait_send()
@@ -347,16 +340,20 @@
         wait_bytes(part.at[0, :, :, pl.ds(0, chips - 1)], rs_send)
 
 
-def _combine_kernel(len_ref, comb_ref, gat_ref, out_ref, ybuf, y_sem):
+def _combine_kernel(reach_ref, comb_ref, gat_ref, out_ref, ybuf, y_sem):
     rows, toks, width = ybuf.shape
-    pos = lax.axis_index("seq") * toks + lax.broadcasted_iota(jnp.int32, (toks, 1), 0)
+    lanes = reach_ref.shape[1]
+    pos = lax.axis_index("seq") * toks + lax.broadcasted_iota(jnp.int32, (toks, lanes), 0)
 
     def out_copy(b):
         return pltpu.make_async_copy(ybuf.at[b], out_ref.at[b], y_sem.at[b])
 
     for b in range(rows):
         acc = jnp.dot(comb_ref[b], gat_ref[b], preferred_element_type=F32)
-        ybuf[b] = jnp.where(pos < len_ref[b], acc, 0.0).astype(BF16)
+        valid = pos < reach_ref[b:b + 1]
+        for i in range(width // lanes):
+            part = slice(i * lanes, (i + 1) * lanes)
+            ybuf[b, :, part] = jnp.where(valid, acc[:, part], 0.0).astype(BF16)
         out_copy(b).start()
     for b in range(rows):
         out_copy(b).wait()
@@ -379,15 +376,16 @@
         dims = (rows, toks, width, slots, seq, experts)
         dma = pltpu.SemaphoreType.DMA
         any_spec = pl.BlockSpec(memory_space=pl.ANY)
-        smem = pl.BlockSpec(memory_space=pltpu.SMEM)
         vmem = pl.BlockSpec(memory_space=pltpu.VMEM)
-        comb, gat = pl.pallas_call(
+        comb, gat, reach = pl.pallas_call(
             functools.partial(_exchange_kernel, dims),
             out_shape=(pltpu.VMEM((rows, toks, slots), BF16),
-                       pltpu.VMEM((rows, HALVES, seq, hs, width), BF16)),
-            in_specs=[smem, smem, any_spec, any_spec, any_spec, any_spec],
-            out_specs=(vmem, vmem),
+                       pltpu.VMEM((rows, HALVES, seq, hs, width), BF16),
+                       pltpu.VMEM((rows, 128), jnp.int32)),
+            in_specs=[any_spec, pl.BlockSpec(memory_space=pltpu.SMEM)] + [any_spec] * 4,
+            out_specs=(vmem, vmem, vmem),
             scratch_shapes=[
+                pltpu.SMEM((rows,), jnp.int32),
                 pltpu.VMEM((rows, toks, width), BF16),
                 pltpu.VMEM((rows, toks, width), BF16),
                 pltpu.VMEM((width, slots), BF16),
@@ -408,9 +406,9 @@
                 pltpu.VMEM((experts, ff, width), BF16),
                 pltpu.VMEM((count // HALVES, width), BF16),
                 pltpu.VMEM((2, slots, toks), BF16),
-                dma((4,)), dma, dma((HALVES,)), dma, dma((groups,)), dma((2,)), dma((2,)),
+                dma((4,)), dma, dma, dma((HALVES,)), dma, dma((groups,)), dma((2,)), dma((2,)),
                 dma((2, groups, HALVES)), dma((HALVES,)), dma,
-                dma((HALVES, CHUNKS, 2, 4)), dma, dma,
+                dma((HALVES, CHUNKS, 4)), dma, dma((CHUNKS,)),
             ],
             compiler_params=pltpu.CompilerParams(
                 collective_id=0, has_side_effects=True, vmem_limit_bytes=VMEM_LIMIT),
@@ -420,12 +418,12 @@
         return pl.pallas_call(
             _combine_kernel,
             out_shape=jax.ShapeDtypeStruct((rows, toks, width), BF16),
-            in_specs=[smem, vmem, vmem],
+            in_specs=[vmem, vmem, vmem],
             out_specs=any_spec,
             scratch_shapes=[pltpu.VMEM((rows, toks, width), BF16), dma((rows,))],
             compiler_params=pltpu.CompilerParams(vmem_limit_bytes=COMBINE_LIMIT),
             name="combine",
-        )(lens, comb, gat)
+        )(reach, comb, gat)
 
     return jax.shard_map(
         shard_body,

time: 47.4 us -> 45.5 us (0.960)
  Pallas kernels: 46.5 us -> 44.6 us
    pallas_call x1, Pallas kernels: 42.6 us -> 41.3 us  [shard_body(): pl.pallas_call(functools.partial(_exchange_kernel, dims), out_shape=(pltp...]
    pallas_call x1, Pallas kernels: 3.84 us -> 3.3 us  [shard_body(): pl.pallas_call(_combine_kernel, out_shape=jax.ShapeDtypeStruct((rows, tok...]
where the time goes in v6:
time: 45.5 us; the launch traced here: 45.4 us
  Pallas kernels  44.6 us (98%)
  between operations  0.82 us (2%)
    pallas_call x1, Pallas kernels, shard_body(): pl.pallas_call(functools.partial(_exchange_kernel, dims), out_shape=(pltp...  41.3 us
    pallas_call x1, Pallas kernels, shard_body(): pl.pallas_call(_combine_kernel, out_shape=jax.ShapeDtypeStruct((rows, tok...  3.3 us

profile of v6, /device:TPU:21, one launch (start us, length us, event | category | flops | bytes accessed | tf_op | source)
XLA Modules:
  0.0 45.4 jit_solution(1899890524131815974)
XLA Ops:
  0.7 41.3 %exchange.1 = (bf16[8,1024,256]{2,1,0:T(8,128)(2,1)S(1)}, bf16[8,2,16,8,384]{4,3,2,1,0:T(8,128)(2,1)S(1)}, s32[8,128]{1,0:T(8,128)S(1)}) custom-call(s32[8]{0:T(128)} %len_hbm.1, f32[1]{0:T(128)S(6)} %copy.7.scale_ref, bf16[384,256]{1,0:T(8,128)(2,1)} %phi_ref.1, bf16[8,1024,384]{2,1,0:T(8,128)(2,1)} %tok_ref.1, bf16[8,384,1536]{2,1,0:T(8,128)(2,1)} %win_ref.1, ...), custom_call_target="tpu_custom_call" | custom-call | tf_op jit(solution)/shard_map/exchange/pallas_call | solution.py:380
  41.9 3.3 %combine.1 = bf16[8,1024,384]{2,1,0:T(8,128)(2,1)} custom-call(s32[8,128]{1,0:T(8,128)S(1)} %get-tuple-element.8.reach_ref, bf16[8,1024,256]{2,1,0:T(8,128)(2,1)S(1)} %get-tuple-element.9.comb_ref, bf16[8,256,384]{2,1,0:T(8,128)(2,1)S(1)} %bitcast.1), custom_call_target="tpu_custom_call" | custom-call | tf_op jit(solution)/shard_map/combine/pallas_call | solution.py:418

commit v7 on v6

--- a/solution.py
+++ b/solution.py
@@ -23,12 +23,13 @@
     ("first", 2, 0), ("relay", 0, 0), ("comb", 0), ("total", 3), ("first", 3, 0), ("first", 3, 1), ("z",),
     ("first", 2, 1), ("comb", 1), ("relay", 1, 0), ("comb", 2), ("relay", 2, 0), ("comb", 3), ("relay", 3, 0),
     ("comb", 4), ("comb", 5), ("relay", 0, 1), ("comb", 6), ("relay", 1, 1), ("relay", 2, 1), ("relay", 3, 1),
-    ("fin", 0), ("ffn", 0), ("dfar", 0, 0), ("dfar", 0, 1), ("dnear", 0, 1), ("fin", 1), ("dnear", 0, 0),
-    ("ffn", 1), ("dfar", 1, 0), ("dfar", 1, 1), ("near", 0, 0), ("fwd", 0, 0), ("fwd", 0, 1), ("near", 0, 1),
-    ("fwd", 1, 0), ("dnear", 1, 1), ("fwd", 1, 1), ("dnear", 1, 0), ("coll", 0, 0), ("comb", 7),
-    ("coll", 1, 0), ("near", 1, 1), ("coll", 0, 1), ("coll", 1, 1), ("near", 1, 0),
+    ("fin", 0), ("ffn", 0), ("dfar", 0, 0), ("dfar", 0, 1), ("dnear", 0, 0), ("dnear", 0, 1), ("fin", 1),
+    ("ffn", 1), ("dfar", 1, 0), ("dfar", 1, 1), ("fwd", 0, 0), ("fwd", 0, 1), ("dnear", 1, 0), ("dnear", 1, 1),
+    ("near", 0, 0), ("near", 0, 1), ("fwd", 1, 0), ("fwd", 1, 1), ("coll", 0, 0), ("coll", 0, 1),
+    ("near", 1, 0), ("near", 1, 1), ("comb", 7), ("coll", 1, 0), ("coll", 1, 1),
 )
 PARTS = 2
+TAIL = 4
 VMEM_LIMIT = 52 * 1024 * 1024
 COMBINE_LIMIT = 20 * 1024 * 1024
 
@@ -247,15 +248,17 @@
         for delta in range(1, chips):
             zsum = zsum + zrecv[delta, h].astype(F32)
         lane = lax.broadcasted_iota(jnp.int32, zsum.shape, 1)
+        zrow = []
+        for b in range(rows):
+            mine = (lane % rows == b) & (lane < 3 * rows)
+            zrow.append(jnp.sum(jnp.where(mine, zsum, 0.0), axis=-1, keepdims=True))
         with jax.named_scope(f"fin{h}"):
             wait_bytes(rbuf.at[:, pl.ds(2, 2), h], fin_recv.at[h])
         for b in range(rows):
             s = chip[b, h, z].astype(F32)
             for way in (UP, DOWN):
                 s = s + (rbuf[way, 2, h, b].astype(F32) + rbuf[way, 3, h, b].astype(F32))
-            mine = (lane % rows == b) & (lane < 3 * rows)
-            zb = jnp.sum(jnp.where(mine, zsum, 0.0), axis=-1, keepdims=True)
-            slot_in[h, b] = s / zb
+            slot_in[h, b] = s / zrow[b]
         inputs = slot_in[h].reshape(rows * hs, width).astype(BF16)
         by_expert[h] = jnp.dot(perm, inputs, preferred_element_type=F32).astype(BF16)
 
@@ -345,18 +348,21 @@
     lanes = reach_ref.shape[1]
     pos = lax.axis_index("seq") * toks + lax.broadcasted_iota(jnp.int32, (toks, lanes), 0)
 
-    def out_copy(b):
-        return pltpu.make_async_copy(ybuf.at[b], out_ref.at[b], y_sem.at[b])
-
-    for b in range(rows):
-        acc = jnp.dot(comb_ref[b], gat_ref[b], preferred_element_type=F32)
-        valid = pos < reach_ref[b:b + 1]
+    pieces = [(b, 0, toks) for b in range(rows - 1)]
+    size = toks // TAIL
+    pieces += [(rows - 1, k * size, size) for k in range(TAIL)]
+    copies = []
+    for n, (b, first, size) in enumerate(pieces):
+        ts = pl.ds(first, size)
+        acc = jnp.dot(comb_ref[b, ts], gat_ref[b], preferred_element_type=F32)
+        valid = pos[first:first + size] < reach_ref[b:b + 1]
         for i in range(width // lanes):
             part = slice(i * lanes, (i + 1) * lanes)
-            ybuf[b, :, part] = jnp.where(valid, acc[:, part], 0.0).astype(BF16)
-        out_copy(b).start()
-    for b in range(rows):
-        out_copy(b).wait()
+            ybuf[b, ts, part] = jnp.where(valid, acc[:, part], 0.0).astype(BF16)
+        copies.append(pltpu.make_async_copy(ybuf.at[b, ts], out_ref.at[b, ts], y_sem.at[n]))
+        copies[-1].start()
+    for copy in copies:
+        copy.wait()
 
 
 def solution(mesh):
@@ -420,7 +426,7 @@
             out_shape=jax.ShapeDtypeStruct((rows, toks, width), BF16),
             in_specs=[vmem, vmem, vmem],
             out_specs=any_spec,
-            scratch_shapes=[pltpu.VMEM((rows, toks, width), BF16), dma((rows,))],
+            scratch_shapes=[pltpu.VMEM((rows, toks, width), BF16), dma((rows - 1 + TAIL,))],
             compiler_params=pltpu.CompilerParams(vmem_limit_bytes=COMBINE_LIMIT),
             name="combine",
         )(reach, comb, gat)

time: 45.5 us -> 45.4 us (level)
  no operation moved by 1% of the time
where the time goes in v7:
time: 45.4 us; the launch traced here: 45.3 us
  Pallas kernels  44.5 us (98%)
  between operations  0.82 us (2%)
    pallas_call x1, Pallas kernels, shard_body(): pl.pallas_call(functools.partial(_exchange_kernel, dims), out_shape=(pltp...  41.2 us
    pallas_call x1, Pallas kernels, shard_body(): pl.pallas_call(_combine_kernel, out_shape=jax.ShapeDtypeStruct((rows, tok...  3.27 us

profile of v7, /device:TPU:21, one launch (start us, length us, event | category | flops | bytes accessed | tf_op | source)
XLA Modules:
  0.0 45.3 jit_solution(15188872527015339530)
XLA Ops:
  0.7 41.2 %exchange.1 = (bf16[8,1024,256]{2,1,0:T(8,128)(2,1)S(1)}, bf16[8,2,16,8,384]{4,3,2,1,0:T(8,128)(2,1)S(1)}, s32[8,128]{1,0:T(8,128)S(1)}) custom-call(s32[8]{0:T(128)} %len_hbm.1, f32[1]{0:T(128)S(6)} %copy.7.scale_ref, bf16[384,256]{1,0:T(8,128)(2,1)} %phi_ref.1, bf16[8,1024,384]{2,1,0:T(8,128)(2,1)} %tok_ref.1, bf16[8,384,1536]{2,1,0:T(8,128)(2,1)} %win_ref.1, ...), custom_call_target="tpu_custom_call" | custom-call | tf_op jit(solution)/shard_map/exchange/pallas_call | solution.py:386
  41.9 3.3 %combine.1 = bf16[8,1024,384]{2,1,0:T(8,128)(2,1)} custom-call(s32[8,128]{1,0:T(8,128)S(1)} %get-tuple-element.8.reach_ref, bf16[8,1024,256]{2,1,0:T(8,128)(2,1)S(1)} %get-tuple-element.9.comb_ref, bf16[8,256,384]{2,1,0:T(8,128)(2,1)S(1)} %bitcast.1), custom_call_target="tpu_custom_call" | custom-call | tf_op jit(solution)/shard_map/combine/pallas_call | solution.py:424

commit v8 on v7

--- a/solution.py
+++ b/solution.py
@@ -25,8 +25,8 @@
     ("comb", 4), ("comb", 5), ("relay", 0, 1), ("comb", 6), ("relay", 1, 1), ("relay", 2, 1), ("relay", 3, 1),
     ("fin", 0), ("ffn", 0), ("dfar", 0, 0), ("dfar", 0, 1), ("dnear", 0, 0), ("dnear", 0, 1), ("fin", 1),
     ("ffn", 1), ("dfar", 1, 0), ("dfar", 1, 1), ("fwd", 0, 0), ("fwd", 0, 1), ("dnear", 1, 0), ("dnear", 1, 1),
-    ("near", 0, 0), ("near", 0, 1), ("fwd", 1, 0), ("fwd", 1, 1), ("coll", 0, 0), ("coll", 0, 1),
-    ("near", 1, 0), ("near", 1, 1), ("comb", 7), ("coll", 1, 0), ("coll", 1, 1),
+    ("near", 0, 0), ("near", 0, 1), ("fwd", 1, 0), ("fwd", 1, 1), ("comb", 7), ("coll", 0, 0), ("coll", 0, 1),
+    ("near", 1, 0), ("near", 1, 1), ("coll", 1, 0), ("coll", 1, 1),
 )
 PARTS = 2
 TAIL = 4

time: 45.4 us -> 45.4 us (level)
  no operation moved by 1% of the time
where the time goes in v8:
time: 45.4 us; the launch traced here: 45.3 us
  Pallas kernels  44.5 us (98%)
  between operations  0.82 us (2%)
    pallas_call x1, Pallas kernels, shard_body(): pl.pallas_call(functools.partial(_exchange_kernel, dims), out_shape=(pltp...  41.2 us
    pallas_call x1, Pallas kernels, shard_body(): pl.pallas_call(_combine_kernel, out_shape=jax.ShapeDtypeStruct((rows, tok...  3.27 us

profile of v8, /device:TPU:21, one launch (start us, length us, event | category | flops | bytes accessed | tf_op | source)
XLA Modules:
  0.0 45.3 jit_solution(4495121084312159549)
XLA Ops:
  0.7 41.2 %exchange.1 = (bf16[8,1024,256]{2,1,0:T(8,128)(2,1)S(1)}, bf16[8,2,16,8,384]{4,3,2,1,0:T(8,128)(2,1)S(1)}, s32[8,128]{1,0:T(8,128)S(1)}) custom-call(s32[8]{0:T(128)} %len_hbm.1, f32[1]{0:T(128)S(6)} %copy.7.scale_ref, bf16[384,256]{1,0:T(8,128)(2,1)} %phi_ref.1, bf16[8,1024,384]{2,1,0:T(8,128)(2,1)} %tok_ref.1, bf16[8,384,1536]{2,1,0:T(8,128)(2,1)} %win_ref.1, ...), custom_call_target="tpu_custom_call" | custom-call | tf_op jit(solution)/shard_map/exchange/pallas_call | solution.py:386
  41.9 3.3 %combine.1 = bf16[8,1024,384]{2,1,0:T(8,128)(2,1)} custom-call(s32[8,128]{1,0:T(8,128)S(1)} %get-tuple-element.8.reach_ref, bf16[8,1024,256]{2,1,0:T(8,128)(2,1)S(1)} %get-tuple-element.9.comb_ref, bf16[8,256,384]{2,1,0:T(8,128)(2,1)S(1)} %bitcast.1), custom_call_target="tpu_custom_call" | custom-call | tf_op jit(solution)/shard_map/combine/pallas_call | solution.py:424
